TPU v7x, 32 devices: a whole 2x2x4 slice. The times are simulated.
32 devices in a mesh: group: 2 (over y), temp: 4 (over x, core), gz: 4 (over z).
Axes of the slice: x: 2, y: 2, z: 4, core: 2. Of those that a mesh axis runs over, the one named last changes fastest.
Arguments:
- spin_state: float32 [16, 3, 16, 128, 128], P(('group', 'temp'), None, 'gz'), parts along dimension 0, may hold values from -1 to 1, as said below
- couplings: float32 [3, 32, 128, 128], P(None, ('group', 'gz')), parts along dimension 1, may hold values from -12 to 12
- inverse_temps: float32 [16], P(('group', 'temp')), parts along dimension 0, may hold values from 0.3 to 3
- colour_order: int32 [16], P(('group', 'temp')), parts along dimension 0, may hold values 0 or 1
- heat_level: float32 [16, 16, 128, 128], P(('group', 'temp'), 'gz'), parts along dimension 0, may hold values from 0.001 to 0.999
- heat_height: float32 [16, 16, 128, 128], P(('group', 'temp'), 'gz'), parts along dimension 0, may hold values from -1 to 1
- heat_angle: float32 [16, 16, 128, 128], P(('group', 'temp'), 'gz'), parts along dimension 0, may hold values from -3.140625 to 3.140625
- swap_bits: int32 [16], P(('group', 'temp')), parts along dimension 0, may hold values 0 or 1
Outputs:
- spin_final: float32 [16, 3, 16, 128, 128], P(('group', 'temp'), None, 'gz'), parts along dimension 0
- energies: float32 [16], P(('group', 'temp')), parts along dimension 0
There are 2 independent parts, one for each index of `group`. A program takes and returns all parts, laid end to end along the dimension named above; each array names one. Nothing has to cross between parts.
Inputs may be any that keep to these rules, and one draw needn't show every extreme that they name: `spin_state`: every site's three components form a vector of unit length.
All inputs are finite; a program needn't handle non-finite values. No bound on the sum of `colour_order` or of `swap_bits` on one device may be relied on, other than what follows from the above.
Results may differ from a plain program's by a relative error of at most 0.0003.
Values sent between devices are 32-bit elements; how exact they have to be, the bound alone decides.
A program may use at most 64 MiB of HBM per device.

v0:
```python
import functools
import math

import jax
import jax.numpy as jnp
from jax import lax
from jax.experimental import pallas as pl
from jax.experimental.pallas import tpu as pltpu
from jax.sharding import PartitionSpec as P

OR_SWEEPS = 2
HALVES = 2 * OR_SWEEPS + 2
PAD = 8
MESH = pl.DeviceIdType.MESH
SIN_TERMS = [(-1.0) ** i / math.factorial(2 * i + 1) for i in range(8)]
COS_TERMS = [(-1.0) ** i / math.factorial(2 * i) for i in range(9)]


def horner(terms, value):
    total = jnp.full_like(value, terms[-1])
    for term in terms[-2::-1]:
        total = total * value + term
    return total


def cos_sin(angle):
    half = 0.5 * angle
    square = half * half
    sine = half * horner(SIN_TERMS, square)
    cosine = horner(COS_TERMS, square)
    return 1.0 - 2.0 * sine * sine, 2.0 * sine * cosine


def dot3(a, b):
    return a[0] * b[0] + a[1] * b[1] + a[2] * b[2]


def reflect(current, pulled):
    factor = 2.0 * dot3(current, pulled) / jnp.maximum(dot3(pulled, pulled), 0.01)
    return [factor * p - s for p, s in zip(pulled, current)]


def heat_bath(pulled, beta, level, trial):
    strength = jnp.sqrt(jnp.maximum(dot3(pulled, pulled), 0.01))
    inverse = 1.0 / strength
    axis = [p * inverse for p in pulled]
    reach = beta * strength
    shrink = -jnp.tanh(reach) * (jnp.exp(-2.0 * reach) + 1.0)
    cosine = 1.0 + jnp.log1p(level * shrink) / reach
    along = dot3(trial, axis)
    tangent = [t - along * a for t, a in zip(trial, axis)]
    scale = jnp.sqrt(jnp.maximum(1.0 - cosine * cosine, 0.0)) * (
        1.0 / jnp.sqrt(jnp.maximum(dot3(tangent, tangent), 0.0001))
    )
    return [cosine * a + scale * t for a, t in zip(axis, tangent)]


def kernel(
    dims,
    spin_hbm,
    coup_hbm,
    beta_ref,
    order_ref,
    level_hbm,
    height_hbm,
    angle_hbm,
    bits_ref,
    out_ref,
    eout_ref,
    spin_in,
    coup_in,
    level_in,
    height_in,
    angle_in,
    lifted,
    sp,
    xo,
    xr,
    yi,
    yo,
    zu,
    zd,
    lv,
    ut,
    eacc,
    ebuf,
    tsend,
    trecv,
    rbuf,
    in_sem,
    hsend,
    hrecv,
    esend,
    erecv,
    tssem,
    trsem,
    xsend,
    xrecv,
):
    count, planes, rows, width, n, m = dims
    k = rows // 2
    chunk = 32 if k % 32 == 0 else 8
    g = lax.axis_index("gz")
    t = lax.axis_index("temp")
    up, down = lax.rem(g + 1, n), lax.rem(g + n - 1, n)
    has_below, has_above = t > 0, t < m - 1

    loads = [
        pltpu.make_async_copy(src, dst, in_sem.at[i])
        for i, (src, dst) in enumerate(
            (
                (spin_hbm.at[:, :, pl.ds(0, 1)], spin_in.at[:, :, pl.ds(0, 1)]),
                (
                    spin_hbm.at[:, :, pl.ds(planes - 1, 1)],
                    spin_in.at[:, :, pl.ds(planes - 1, 1)],
                ),
                (coup_hbm.at[2, planes - 1], coup_in.at[2, planes - 1]),
                (coup_hbm.at[pl.ds(0, 2)], coup_in.at[pl.ds(0, 2)]),
                (
                    coup_hbm.at[2, pl.ds(0, planes - 1)],
                    coup_in.at[2, pl.ds(0, planes - 1)],
                ),
                (
                    spin_hbm.at[:, :, pl.ds(1, planes - 2)],
                    spin_in.at[:, :, pl.ds(1, planes - 2)],
                ),
                (level_hbm, level_in),
                (height_hbm, height_in),
                (angle_hbm, angle_in),
            )
        )
    ]
    for load in loads:
        load.start()

    barrier = pltpu.get_barrier_semaphore()
    for d in range(1, n):
        pl.semaphore_signal(
            barrier, inc=1, device_id={"gz": lax.rem(g + d, n)}, device_id_type=MESH
        )

    @pl.when(has_below)
    def _():
        pl.semaphore_signal(barrier, inc=1, device_id={"temp": t - 1}, device_id_type=MESH)

    @pl.when(has_above)
    def _():
        pl.semaphore_signal(barrier, inc=1, device_id={"temp": t + 1}, device_id_type=MESH)

    pl.semaphore_wait(barrier, n - 1 + has_below.astype(jnp.int32) + has_above.astype(jnp.int32))

    def parity(r, z, size):
        lane = lax.broadcasted_iota(jnp.int32, (size, width), 1)
        return ((lane + (g * planes + z + order_ref[r])) & 1) != 0

    def halves(ref, index, start, size):
        even = ref[index + (pl.ds(2 * start, size, stride=2), slice(None))]
        odd = ref[index + (pl.ds(2 * start + 1, size, stride=2), slice(None))]
        return even, odd

    def put_spin(c, r, d, z, start, value):
        size = value.shape[0]
        sp[c, r, d, z + 1, pl.ds(PAD + start, size), :] = value
        if start == 0:
            sp[c, r, d, z + 1, pl.ds(PAD + k, 1), :] = value[0:1]
        if start + size == k:
            sp[c, r, d, z + 1, pl.ds(PAD - 1, 1), :] = value[size - 1 : size]

    def pack_spin(r, z):
        e = parity(r, z, k)
        for d in range(3):
            even, odd = halves(spin_in, (r, d, z), 0, k)
            put_spin(0, r, d, z, 0, jnp.where(e, odd, even))
            put_spin(1, r, d, z, 0, jnp.where(e, even, odd))

    def halo(x, r, side):
        c = 1 - x % 2
        plain = sp.at[c, r, :, 1, pl.ds(PAD, k), :]
        return pltpu.make_async_remote_copy(
            src_ref=plain if side == 0 else lifted.at[c, r],
            dst_ref=sp.at[c, r, :, planes + 1 if side == 0 else 0, pl.ds(PAD, k), :],
            send_sem=hsend.at[x, r, side],
            recv_sem=hrecv.at[x, r, side],
            device_id={"gz": down if side == 0 else up},
            device_id_type=MESH,
        )

    def lift(c, r, d, start, value):
        part = pl.ds(start, value.shape[0])
        lifted[c, r, d, part, :] = zu[c, r, planes - 1, part, :] * value

    def inner(action):
        def step(i, carry):
            action(i // (planes - 2), 1 + i % (planes - 2))
            return carry

        if planes > 2:
            lax.fori_loop(0, count * (planes - 2), step, 0)

    for load in loads[:3]:
        load.wait()
    for r in range(count):
        pack_spin(r, 0)
        halo(0, r, 0).start()
        e = parity(r, planes - 1, k)
        even, odd = halves(coup_in, (2, planes - 1), 0, k)
        zu[0, r, planes - 1] = jnp.where(e, odd, even)
        zu[1, r, planes - 1] = jnp.where(e, even, odd)
        pack_spin(r, planes - 1)
        for d in range(3):
            lift(1, r, d, 0, sp[1, r, d, planes, pl.ds(PAD, k), :])
        halo(0, r, 1).start()
    for load in loads[3:6]:
        load.wait()
    inner(pack_spin)

    def pack_bonds(i, carry):
        r, z = i // planes, i % planes
        e = parity(r, z, k)
        even, odd = halves(coup_in, (0, z), 0, k)
        first, second = jnp.where(e, odd, even), jnp.where(e, even, odd)
        xo[0, r, z] = first
        xo[1, r, z] = second
        xr[0, r, z] = pltpu.roll(second, 1, 1)
        xr[1, r, z] = pltpu.roll(first, 1, 1)
        even, odd = halves(coup_in, (1, z), 0, k)
        before = pltpu.roll(odd, 1, 0)
        yi[r, z] = even
        yo[0, r, z] = jnp.where(e, odd, before)
        yo[1, r, z] = jnp.where(e, before, odd)
        return carry

    def pack_lower(i, carry):
        r, z = i // (planes - 1), 1 + i % (planes - 1)
        e = parity(r, z, k)
        even, odd = halves(coup_in, (2, z - 1), 0, k)
        zd[0, r, z] = jnp.where(e, odd, even)
        zd[1, r, z] = jnp.where(e, even, odd)
        zu[0, r, z - 1] = jnp.where(e, even, odd)
        zu[1, r, z - 1] = jnp.where(e, odd, even)
        return carry

    lax.fori_loop(0, count * planes, pack_bonds, 0)
    lax.fori_loop(0, count * (planes - 1), pack_lower, 0)
    for r in range(count):
        for c in (0, 1):
            zd[c, r, 0] = jnp.ones((k, width), jnp.float32)

    def pull(c, r, z, start):
        o = 1 - c
        part = pl.ds(start, chunk)
        e = parity(r, z, chunk)
        bx, br, by = xo[c, r, z, part, :], xr[c, r, z, part, :], yi[r, z, part, :]
        bo, bu, bd = yo[c, r, z, part, :], zu[c, r, z, part, :], zd[c, r, z, part, :]
        pulled = []
        for d in range(3):
            mid = sp[o, r, d, z + 1, pl.ds(PAD + start, chunk), :]
            nxt = sp[o, r, d, z + 1, pl.ds(PAD + start + 1, chunk), :]
            prv = sp[o, r, d, z + 1, pl.ds(PAD + start - 1, chunk), :]
            outer = jnp.where(e, nxt, prv) if c == 0 else jnp.where(e, prv, nxt)
            total = bx * pltpu.roll(mid, width - 1, 1) + br * pltpu.roll(mid, 1, 1)
            total = total + by * mid + bo * outer
            total = total + bu * sp[o, r, d, z + 2, pl.ds(PAD + start, chunk), :]
            total = total + bd * sp[o, r, d, z, pl.ds(PAD + start, chunk), :]
            pulled.append(total)
        return pulled

    def relax(c, r, z, lifting=False):
        for start in range(0, k, chunk):
            pulled = pull(c, r, z, start)
            current = [sp[c, r, d, z + 1, pl.ds(PAD + start, chunk), :] for d in range(3)]
            for d, value in enumerate(reflect(current, pulled)):
                put_spin(c, r, d, z, start, value)
                if lifting:
                    lift(c, r, d, start, value)

    def heat(c, r, z, lifting=False):
        for start in range(0, k, chunk):
            part = pl.ds(start, chunk)
            pulled = pull(c, r, z, start)
            trial = [ut[c, r, d, z, part, :] for d in range(3)]
            renewed = heat_bath(pulled, beta_ref[r], lv[c, r, z, part, :], trial)
            for d, value in enumerate(renewed):
                put_spin(c, r, d, z, start, value)
                if lifting:
                    lift(c, r, d, start, value)
            if c == 1:
                terms = dot3(renewed, pulled)
                eacc[r] = eacc[r] + sum(terms[j : j + 8] for j in range(0, chunk, 8))

    def pack_heat(r):
        def step(z, carry):
            for start in range(0, k, chunk):
                part = pl.ds(start, chunk)
                e = parity(r, z, chunk)
                even, odd = halves(level_in, (r, z), start, chunk)
                lv[0, r, z, part, :] = jnp.where(e, odd, even)
                lv[1, r, z, part, :] = jnp.where(e, even, odd)
                angles = halves(angle_in, (r, z), start, chunk)
                heights = halves(height_in, (r, z), start, chunk)
                trials = []
                for angle, height in zip(angles, heights):
                    side = jnp.sqrt(jnp.maximum(1.0 - height * height, 0.0))
                    cosine, sine = cos_sin(angle)
                    trials.append((side * cosine, side * sine, height))
                for d in range(3):
                    ut[0, r, d, z, part, :] = jnp.where(e, trials[1][d], trials[0][d])
                    ut[1, r, d, z, part, :] = jnp.where(e, trials[0][d], trials[1][d])
            return carry

        lax.fori_loop(0, planes, step, 0)

    def take_halo(x, r, side):
        halo(x, r, 1 - side).wait_recv()
        if x >= 1:
            halo(x - 1, r, side).wait_send()

    eacc[...] = jnp.zeros_like(eacc)
    for x in range(HALVES - 1):
        c = x % 2
        work = functools.partial(relax if x < 2 * OR_SWEEPS else heat, c)
        for r in range(count):
            for side, z in ((0, 0), (1, planes - 1)):
                take_halo(x, r, side)
                work(r, z, lifting=side == 1)
                halo(x + 1, r, side).start()
        inner(work)
        if x == 0:
            for load in loads[6:]:
                load.wait()
        for r in range(count):
            if r % (2 * OR_SWEEPS) == x:
                pack_heat(r)

    def flag(j, size):
        return jnp.full((size, width), bits_ref[j], jnp.int32) != 0

    def unpack(z):
        for r in range(0, count, 2):
            taking = flag(r, k)
            masks = [parity(r + j, z, k) for j in (0, 1)]
            for d in range(3):
                both = []
                for j in (0, 1):
                    first = sp[0, r + j, d, z + 1, pl.ds(PAD, k), :]
                    second = sp[1, r + j, d, z + 1, pl.ds(PAD, k), :]
                    both.append(
                        (jnp.where(masks[j], second, first), jnp.where(masks[j], first, second))
                    )
                for row in (0, 1):
                    low, top = both[0][row], both[1][row]
                    place = pl.ds(row, k, stride=2)
                    out_ref[r, d, z, place, :] = jnp.where(taking, top, low)
                    out_ref[r + 1, d, z, place, :] = jnp.where(taking, low, top)

    def ship(z, side):
        return pltpu.make_async_remote_copy(
            src_ref=out_ref.at[count - 1 if side == 0 else 0, :, z],
            dst_ref=rbuf.at[side, :, z],
            send_sem=xsend.at[z, side],
            recv_sem=xrecv.at[z, side],
            device_id={"temp": t + 1 if side == 0 else t - 1},
            device_id_type=MESH,
        )

    def finish(plane_list):
        for z in plane_list:
            unpack(z)

            @pl.when(has_above)
            def _():
                ship(z, 0).start()

            @pl.when(has_below)
            def _():
                ship(z, 1).start()

    x = HALVES - 1
    work = functools.partial(heat, 1)
    inner(work)
    middle = list(range(1, planes - 1))
    outside = [0, planes - 1]
    finish(middle)
    for side, z in ((0, 0), (1, planes - 1)):
        for r in range(count):
            take_halo(x, r, side)
            work(r, z)
        if side == 0:
            finish([z])
    swaps = []
    for d in range(1, n):
        swaps.append(
            pltpu.make_async_remote_copy(
                src_ref=eacc,
                dst_ref=ebuf.at[d - 1],
                send_sem=esend.at[d - 1],
                recv_sem=erecv.at[d - 1],
                device_id={"gz": lax.rem(g + d, n)},
                device_id_type=MESH,
            )
        )
    for swap in swaps:
        swap.start()
    finish([planes - 1])

    for swap in swaps:
        swap.wait()
    sites = float(width * rows * planes * n)
    energy = []
    for r in range(count):
        total = eacc[r]
        for d in range(n - 1):
            total = total + ebuf[d, r]
        summed = jnp.sum(jnp.sum(total, axis=0, keepdims=True), axis=1, keepdims=True)
        energy.append(jnp.broadcast_to(-summed / sites, (8, width)))
    for r in range(0, count, 2):
        taking = flag(r, 8)
        low, top = energy[r], energy[r + 1]
        energy[r], energy[r + 1] = jnp.where(taking, top, low), jnp.where(taking, low, top)
    tsend[0] = energy[count - 1]
    tsend[1] = jnp.full((8, width), bits_ref[count - 1], jnp.int32).astype(jnp.float32)
    tsend[2] = energy[0]

    def tell(side):
        part = pl.ds(0, 2) if side == 0 else pl.ds(2, 1)
        return pltpu.make_async_remote_copy(
            src_ref=tsend.at[part],
            dst_ref=trecv.at[part],
            send_sem=tssem.at[side],
            recv_sem=trsem.at[side],
            device_id={"temp": t + 1 if side == 0 else t - 1},
            device_id_type=MESH,
        )

    @pl.when(has_above)
    def _():
        tell(0).start()

    @pl.when(has_below)
    def _():
        tell(1).start()

    for r in range(1, count - 1, 2):
        taking = flag(r, 8)
        low, top = energy[r], energy[r + 1]
        energy[r], energy[r + 1] = jnp.where(taking, top, low), jnp.where(taking, low, top)
        wide = flag(r, rows)

        def exchange(i, carry):
            d, z = i // planes, i % planes
            a, b = out_ref[r, d, z], out_ref[r + 1, d, z]
            out_ref[r, d, z] = jnp.where(wide, b, a)
            out_ref[r + 1, d, z] = jnp.where(wide, a, b)
            return carry

        lax.fori_loop(0, 3 * planes, exchange, 0)

    for r in range(count):
        eout_ref[r] = jnp.max(energy[r])

    for r in range(count):
        for side in (0, 1):
            halo(x, r, side).wait_send()

    @pl.when(has_above)
    def _():
        tell(0).wait_send()
        tell(1).wait_recv()
        wide = flag(count - 1, rows)
        eout_ref[count - 1] = jnp.max(
            jnp.where(flag(count - 1, 8), trecv[2], energy[count - 1])
        )
        for z in middle + outside:
            ship(z, 0).wait_send()
            ship(z, 1).wait_recv()
            for d in range(3):
                out_ref[count - 1, d, z] = jnp.where(wide, rbuf[1, d, z], out_ref[count - 1, d, z])

    @pl.when(has_below)
    def _():
        tell(1).wait_send()
        tell(0).wait_recv()
        eout_ref[0] = jnp.max(jnp.where(trecv[1] > 0.5, trecv[0], energy[0]))
        wide = jnp.broadcast_to(trecv[1][0:1], (rows, width)) > 0.5
        for z in middle + outside:
            ship(z, 1).wait_send()
            ship(z, 0).wait_recv()
            for d in range(3):
                out_ref[0, d, z] = jnp.where(wide, rbuf[0, d, z], out_ref[0, d, z])


def on_device(n, m, spin, coup, beta, order, level, height, angle, bits):
    count, _, planes, rows, width = spin.shape
    k = rows // 2
    f32 = jnp.float32
    hbm = pl.BlockSpec(memory_space=pltpu.HBM)
    smem = pl.BlockSpec(memory_space=pltpu.SMEM)
    dma = pltpu.SemaphoreType.DMA
    bonds = pltpu.VMEM((2, count, planes, k, width), f32)
    return pl.pallas_call(
        functools.partial(kernel, (count, planes, rows, width, n, m)),
        out_shape=(
            jax.ShapeDtypeStruct(spin.shape, f32),
            jax.ShapeDtypeStruct((count,), f32),
        ),
        in_specs=[hbm, hbm, smem, smem, hbm, hbm, hbm, smem],
        out_specs=(pl.BlockSpec(memory_space=pltpu.VMEM), smem),
        scratch_shapes=[
            pltpu.VMEM(spin.shape, f32),
            pltpu.VMEM(coup.shape, f32),
            pltpu.VMEM(level.shape, f32),
            pltpu.VMEM(level.shape, f32),
            pltpu.VMEM(level.shape, f32),
            pltpu.VMEM((2, count, 3, k, width), f32),
            pltpu.VMEM((2, count, 3, planes + 2, k + 2 * PAD, width), f32),
            bonds,
            bonds,
            pltpu.VMEM((count, planes, k, width), f32),
            bonds,
            bonds,
            bonds,
            bonds,
            pltpu.VMEM((2, count, 3, planes, k, width), f32),
            pltpu.VMEM((count, 8, width), f32),
            pltpu.VMEM((n - 1, count, 8, width), f32),
            pltpu.VMEM((3, 8, width), f32),
            pltpu.VMEM((3, 8, width), f32),
            pltpu.VMEM((2, 3, planes, rows, width), f32),
            dma((9,)),
            dma((HALVES, count, 2)),
            dma((HALVES, count, 2)),
            dma((n - 1,)),
            dma((n - 1,)),
            dma((2,)),
            dma((2,)),
            dma((planes, 2)),
            dma((planes, 2)),
        ],
        compiler_params=pltpu.CompilerParams(
            collective_id=0, has_side_effects=True, vmem_limit_bytes=60 * 1024 * 1024
        ),
    )(spin, coup, beta, order, level, height, angle, bits)


def solution(mesh):
    n, m = mesh.shape["gz"], mesh.shape["temp"]
    return jax.shard_map(
        functools.partial(on_device, n, m),
        mesh=mesh,
        in_specs=(
            P(("group", "temp"), None, "gz", None, None),
            P(None, ("group", "gz"), None, None),
            P(("group", "temp")),
            P(("group", "temp")),
            P(("group", "temp"), "gz", None, None),
            P(("group", "temp"), "gz", None, None),
            P(("group", "temp"), "gz", None, None),
            P(("group", "temp")),
        ),
        out_specs=(P(("group", "temp"), None, "gz", None, None), P(("group", "temp"))),
        check_vma=False,
    )
```

profile of v0, /device:TPU:1, one launch (start us, length us, event | category | flops | bytes accessed | tf_op | source)
XLA Modules:
  0.0 71.2 jit_solution(18080509525212447783)
XLA Ops:
  0.6 67.4 %shard_map.95 = (f32[2,3,4,128,128]{4,3,2,1,0:T(8,128)}, f32[2]{0:T(128)}) custom-call(f32[2,3,4,128,128]{4,3,2,1,0:T(8,128)} %spin_hbm.1, f32[3,4,128,128]{3,2,1,0:T(8,128)} %coup_hbm.1, f32[2]{0:T(128)} %beta_ref.1, s32[2]{0:T(128)} %order_ref.1, f32[2,4,128,128]{3,2,1,0:T(8,128)} %level_hbm.1, f32[2,4,128,128]{3,2,1,0:T(8,128)} %height_hbm.1, ...), custom_call_target="tpu_custom_call" | custom-call | tf_op jit(solution)/shard_map/pallas_call | solution.py:500
  68.0 0.0 copy-start
  68.0 2.7 %copy.12 = f32[2,3,4,128,128]{4,3,2,1,0:T(8,128)} copy(f32[2,3,4,128,128]{4,3,2,1,0:T(8,128)} %get-tuple-element.4) | data formatting | bytes 3145728
  70.7 0.0 copy-done
  70.7 0.5 copy.13
Async XLA Ops:
  68.0 2.7 %copy-start = (f32[2]{0:T(128)S(1)}, f32[2]{0:T(128)}, u32[]{:S(2)}) copy-start(f32[2]{0:T(128)} %get-tuple-element.5) | copy-start | bytes 28
where the time goes:
time: 71.4 us; the launch traced here: 71.2 us
  Pallas kernels  67.4 us (94%)
  local copies, waits for them, and re-layouts  3.22 us (5%)
    pallas_call x1, Pallas kernels, on_device(): pl.pallas_call(functools.partial(kernel, (count, planes, rows, width, n,...  67.4 us
    unnamed x4, local copies, waits for them, and re-layouts  3.22 us

commit v1 on v0

v1 whole, which is shorter than its diff:
```python
import functools
import math

import jax
import jax.numpy as jnp
from jax import lax
from jax.experimental import pallas as pl
from jax.experimental.pallas import tpu as pltpu
from jax.sharding import PartitionSpec as P

OR_SWEEPS = 2
HALVES = 2 * OR_SWEEPS + 2
PAD = 8
MESH = pl.DeviceIdType.MESH
SIN_TERMS = [(-1.0) ** i / math.factorial(2 * i + 1) for i in range(8)]
COS_TERMS = [(-1.0) ** i / math.factorial(2 * i) for i in range(9)]


def horner(terms, value):
    total = jnp.full_like(value, terms[-1])
    for term in terms[-2::-1]:
        total = total * value + term
    return total


def cos_sin(angle):
    half = 0.5 * angle
    square = half * half
    sine = half * horner(SIN_TERMS, square)
    cosine = horner(COS_TERMS, square)
    return 1.0 - 2.0 * sine * sine, 2.0 * sine * cosine


def dot3(a, b):
    return a[0] * b[0] + a[1] * b[1] + a[2] * b[2]


def reflect(current, pulled):
    factor = 2.0 * dot3(current, pulled) / jnp.maximum(dot3(pulled, pulled), 0.01)
    return [factor * p - s for p, s in zip(pulled, current)]


def heat_bath(pulled, beta, level, trial):
    strength = jnp.sqrt(jnp.maximum(dot3(pulled, pulled), 0.01))
    inverse = 1.0 / strength
    axis = [p * inverse for p in pulled]
    reach = beta * strength
    shrink = -jnp.tanh(reach) * (jnp.exp(-2.0 * reach) + 1.0)
    cosine = 1.0 + jnp.log1p(level * shrink) / reach
    along = dot3(trial, axis)
    tangent = [t - along * a for t, a in zip(trial, axis)]
    scale = jnp.sqrt(jnp.maximum(1.0 - cosine * cosine, 0.0)) * (
        1.0 / jnp.sqrt(jnp.maximum(dot3(tangent, tangent), 0.0001))
    )
    return [cosine * a + scale * t for a, t in zip(axis, tangent)]


def flag(bits_ref, j, size, width):
    return jnp.full((size, width), bits_ref[j], jnp.int32) != 0


def sweep_kernel(
    dims,
    spin_hbm,
    coup_hbm,
    beta_ref,
    order_ref,
    level_hbm,
    height_hbm,
    angle_hbm,
    bits_ref,
    evened,
    rbuf,
    trecv,
    ebuf,
    spin_in,
    coup_in,
    level_in,
    height_in,
    angle_in,
    lifted,
    sp,
    xo,
    xr,
    yi,
    yo,
    zu,
    zd,
    lv,
    ut,
    eacc,
    tsend,
    in_sem,
    hsend,
    hrecv,
    esend,
    erecv,
    tssem,
    trsem,
    xsend,
    xrecv,
    wrap_sem,
):
    count, planes, rows, width, n, m = dims
    k = rows // 2
    chunk = 32 if k % 32 == 0 else 8
    last = planes - 1
    g = lax.axis_index("gz")
    t = lax.axis_index("temp")
    up, down = lax.rem(g + 1, n), lax.rem(g + n - 1, n)
    has_below, has_above = t > 0, t < m - 1
    near = 2 < n <= 2 * HALVES - 2

    loads = [
        pltpu.make_async_copy(src, dst, in_sem.at[i])
        for i, (src, dst) in enumerate(
            (
                (spin_hbm.at[:, :, pl.ds(0, 1)], spin_in.at[:, :, pl.ds(0, 1)]),
                (spin_hbm.at[:, :, pl.ds(last, 1)], spin_in.at[:, :, pl.ds(last, 1)]),
                (coup_hbm.at[2, last], coup_in.at[2, last]),
                (coup_hbm.at[pl.ds(0, 2)], coup_in.at[pl.ds(0, 2)]),
                (coup_hbm.at[2, pl.ds(0, last)], coup_in.at[2, pl.ds(0, last)]),
                (
                    spin_hbm.at[:, :, pl.ds(1, planes - 2)],
                    spin_in.at[:, :, pl.ds(1, planes - 2)],
                ),
                (level_hbm, level_in),
                (height_hbm, height_in),
                (angle_hbm, angle_in),
            )
        )
    ]

    def peer(dt, there):
        return {"gz": there} if dt == 0 else {"temp": t + dt, "gz": there}

    def along(dt, action):
        if dt == 0:
            action()
        else:
            pl.when(has_below if dt < 0 else has_above)(action)

    barrier = pltpu.get_barrier_semaphore()

    def greet(dt, there):
        pl.semaphore_signal(barrier, inc=1, device_id=peer(dt, there), device_id_type=MESH)

    sides = has_below.astype(jnp.int32) + has_above.astype(jnp.int32)
    if near:

        @pl.when(g < n - 1)
        def _():
            greet(0, up)

        greet(0, down)
        along(-1, lambda: greet(-1, g))
        along(1, lambda: greet(1, g))
        expected = sides + jnp.where(g == 0, 1, 2)
    else:
        for dt in (-1, 0, 1):

            def greet_all(dt=dt):
                for d in range(1 if dt == 0 else 0, n):
                    greet(dt, lax.rem(g + d, n))

            along(dt, greet_all)
        expected = n - 1 + n * sides

    for load in loads:
        load.start()

    def parity(r, z, size):
        lane = lax.broadcasted_iota(jnp.int32, (size, width), 1)
        return ((lane + (g * planes + z + order_ref[r])) & 1) != 0

    def halves(ref, index, start, size):
        even = ref[index + (pl.ds(2 * start, size, stride=2), slice(None))]
        odd = ref[index + (pl.ds(2 * start + 1, size, stride=2), slice(None))]
        return even, odd

    def put_spin(c, r, d, z, start, value):
        size = value.shape[0]
        sp[c, r, d, z + 1, pl.ds(PAD + start, size), :] = value
        if start == 0:
            sp[c, r, d, z + 1, pl.ds(PAD + k, 1), :] = value[0:1]
        if start + size == k:
            sp[c, r, d, z + 1, pl.ds(PAD - 1, 1), :] = value[size - 1 : size]

    def pack_spin(r, z):
        e = parity(r, z, k)
        for d in range(3):
            even, odd = halves(spin_in, (r, d, z), 0, k)
            put_spin(0, r, d, z, 0, jnp.where(e, odd, even))
            put_spin(1, r, d, z, 0, jnp.where(e, even, odd))

    def halo(x, r, side):
        c = 1 - x % 2
        plain = sp.at[c, r, :, 1, pl.ds(PAD, k), :]
        return pltpu.make_async_remote_copy(
            src_ref=plain if side == 0 else lifted.at[c, r],
            dst_ref=sp.at[c, r, :, planes + 1 if side == 0 else 0, pl.ds(PAD, k), :],
            send_sem=hsend.at[x, r, side],
            recv_sem=hrecv.at[x, r, side],
            device_id={"gz": down if side == 0 else up},
            device_id_type=MESH,
        )

    def lift(c, r, d, start, value):
        part = pl.ds(start, value.shape[0])
        lifted[c, r, d, part, :] = zu[c, r, last, part, :] * value

    def inner(r, action):
        if planes > 2:
            lax.fori_loop(1, last, lambda z, carry: (action(r, z), carry)[1], 0)

    for load in loads[:3]:
        load.wait()
    for r in range(count):
        e = parity(r, last, k)
        even, odd = halves(coup_in, (2, last), 0, k)
        zu[0, r, last] = jnp.where(e, odd, even)
        zu[1, r, last] = jnp.where(e, even, odd)
        pack_spin(r, last)
        for d in range(3):
            lift(1, r, d, 0, sp[1, r, d, planes, pl.ds(PAD, k), :])
        pack_spin(r, 0)

    def slot_order(r):
        other = order_ref[r ^ 1]
        return jnp.where(bits_ref[r - r % 2] != 0, other, order_ref[r])

    def wide(value):
        return jnp.full((1, width), value, jnp.int32).astype(jnp.float32)

    tsend[0, 0:1] = wide(slot_order(count - 1))
    tsend[0, 1:2] = wide(bits_ref[count - 1])
    tsend[0, 2:3] = wide(bits_ref[count - 2])
    tsend[1, 0:1] = wide(slot_order(0))
    tsend[1, 1:2] = wide(0)
    tsend[1, 2:3] = wide(bits_ref[0])
    for r in range(count):
        trecv[2, r : r + 1] = wide(slot_order(r))
        trecv[2, count + r : count + r + 1] = wide(bits_ref[r])

    pl.semaphore_wait(barrier, expected)
    if near:

        @pl.when(g == n - 1)
        def _():
            pl.semaphore_signal(wrap_sem, inc=1, device_id={"gz": up}, device_id_type=MESH)

    for r in range(count):
        halo(0, r, 1).start()
        if r == 0 and near:

            @pl.when(g == 0)
            def _():
                pl.semaphore_wait(wrap_sem, 1)

        halo(0, r, 0).start()

    def tell(side):
        return pltpu.make_async_remote_copy(
            src_ref=tsend.at[side],
            dst_ref=trecv.at[side],
            send_sem=tssem.at[side],
            recv_sem=trsem.at[side],
            device_id={"temp": t + 1 if side == 0 else t - 1},
            device_id_type=MESH,
        )

    along(1, lambda: tell(0).start())
    along(-1, lambda: tell(1).start())

    for load in loads[3:6]:
        load.wait()

    def pack_bonds(i, carry):
        r, z = i // planes, i % planes
        e = parity(r, z, k)
        even, odd = halves(coup_in, (0, z), 0, k)
        first, second = jnp.where(e, odd, even), jnp.where(e, even, odd)
        xo[0, r, z] = first
        xo[1, r, z] = second
        xr[0, r, z] = pltpu.roll(second, 1, 1)
        xr[1, r, z] = pltpu.roll(first, 1, 1)
        even, odd = halves(coup_in, (1, z), 0, k)
        before = pltpu.roll(odd, 1, 0)
        yi[r, z] = even
        yo[0, r, z] = jnp.where(e, odd, before)
        yo[1, r, z] = jnp.where(e, before, odd)
        return carry

    def pack_lower(i, carry):
        r, z = i // last, 1 + i % last
        e = parity(r, z, k)
        even, odd = halves(coup_in, (2, z - 1), 0, k)
        zd[0, r, z] = jnp.where(e, odd, even)
        zd[1, r, z] = jnp.where(e, even, odd)
        zu[0, r, z - 1] = jnp.where(e, even, odd)
        zu[1, r, z - 1] = jnp.where(e, odd, even)
        return carry

    for r in range(count):
        inner(r, pack_spin)
    lax.fori_loop(0, count * planes, pack_bonds, 0)
    lax.fori_loop(0, count * last, pack_lower, 0)
    for r in range(count):
        for c in (0, 1):
            zd[c, r, 0] = jnp.ones((k, width), jnp.float32)

    def pull(c, r, z, start):
        o = 1 - c
        part = pl.ds(start, chunk)
        e = parity(r, z, chunk)
        bx, br, by = xo[c, r, z, part, :], xr[c, r, z, part, :], yi[r, z, part, :]
        bo, bu, bd = yo[c, r, z, part, :], zu[c, r, z, part, :], zd[c, r, z, part, :]
        pulled = []
        for d in range(3):
            mid = sp[o, r, d, z + 1, pl.ds(PAD + start, chunk), :]
            nxt = sp[o, r, d, z + 1, pl.ds(PAD + start + 1, chunk), :]
            prv = sp[o, r, d, z + 1, pl.ds(PAD + start - 1, chunk), :]
            outer = jnp.where(e, nxt, prv) if c == 0 else jnp.where(e, prv, nxt)
            total = bx * pltpu.roll(mid, width - 1, 1) + br * pltpu.roll(mid, 1, 1)
            total = total + by * mid + bo * outer
            total = total + bu * sp[o, r, d, z + 2, pl.ds(PAD + start, chunk), :]
            total = total + bd * sp[o, r, d, z, pl.ds(PAD + start, chunk), :]
            pulled.append(total)
        return pulled

    def relax(c, r, z, lifting=False):
        for start in range(0, k, chunk):
            pulled = pull(c, r, z, start)
            current = [sp[c, r, d, z + 1, pl.ds(PAD + start, chunk), :] for d in range(3)]
            for d, value in enumerate(reflect(current, pulled)):
                put_spin(c, r, d, z, start, value)
                if lifting:
                    lift(c, r, d, start, value)

    def heat(c, r, z, lifting=False):
        for start in range(0, k, chunk):
            part = pl.ds(start, chunk)
            pulled = pull(c, r, z, start)
            trial = [ut[c, r, d, z, part, :] for d in range(3)]
            renewed = heat_bath(pulled, beta_ref[r], lv[c, r, z, part, :], trial)
            for d, value in enumerate(renewed):
                put_spin(c, r, d, z, start, value)
                if lifting:
                    lift(c, r, d, start, value)
            if c == 1:
                terms = dot3(renewed, pulled)
                eacc[r] = eacc[r] + sum(terms[j : j + 8] for j in range(0, chunk, 8))

    def pack_heat(r, z):
        for start in range(0, k, chunk):
            part = pl.ds(start, chunk)
            e = parity(r, z, chunk)
            even, odd = halves(level_in, (r, z), start, chunk)
            lv[0, r, z, part, :] = jnp.where(e, odd, even)
            lv[1, r, z, part, :] = jnp.where(e, even, odd)
            angles = halves(angle_in, (r, z), start, chunk)
            heights = halves(height_in, (r, z), start, chunk)
            trials = []
            for angle, height in zip(angles, heights):
                side = jnp.sqrt(jnp.maximum(1.0 - height * height, 0.0))
                cosine, sine = cos_sin(angle)
                trials.append((side * cosine, side * sine, height))
            for d in range(3):
                ut[0, r, d, z, part, :] = jnp.where(e, trials[1][d], trials[0][d])
                ut[1, r, d, z, part, :] = jnp.where(e, trials[0][d], trials[1][d])

    def take_halo(x, r, side):
        halo(x, r, 1 - side).wait_recv()
        if x >= 1:
            halo(x - 1, r, side).wait_send()

    eacc[...] = jnp.zeros_like(eacc)
    relaxing = 2 * OR_SWEEPS
    for x in range(HALVES - 1):
        c = x % 2
        work = functools.partial(relax if x < relaxing else heat, c)
        for r in range(count):
            for side, z in ((0, 0), (1, last)):
                take_halo(x, r, side)
                work(r, z, lifting=side == 1)
                halo(x + 1, r, side).start()
            inner(r, work)
            if x == 0 and r == 0:
                for load in loads[6:]:
                    load.wait()
            for z in range(planes):
                if z % relaxing == x:
                    pack_heat(r, z)

    def settle(c, z):
        for r in range(0, count, 2):
            taking = flag(bits_ref, r, k, width)
            for d in range(3):
                low = sp[c, r, d, z + 1, pl.ds(PAD, k), :]
                top = sp[c, r + 1, d, z + 1, pl.ds(PAD, k), :]
                evened[r, c, z, d] = jnp.where(taking, top, low)
                evened[r + 1, c, z, d] = jnp.where(taking, low, top)

    def ship(c, z, side):
        return pltpu.make_async_remote_copy(
            src_ref=evened.at[count - 1 if side == 0 else 0, c, z],
            dst_ref=rbuf.at[side, c, z],
            send_sem=xsend.at[c, z, side],
            recv_sem=xrecv.at[c, z, side],
            device_id={"temp": t + 1 if side == 0 else t - 1},
            device_id_type=MESH,
        )

    def send_off(c, z):
        settle(c, z)
        along(1, lambda: ship(c, z, 0).start())
        along(-1, lambda: ship(c, z, 1).start())

    x = HALVES - 1
    work = functools.partial(heat, 1)
    for z in range(planes):
        send_off(0, z)
    for r in range(count):
        inner(r, work)
    for z in range(1, last):
        send_off(1, z)
    for r in range(count):
        for side, z in ((0, 0), (1, last)):
            take_halo(x, r, side)
            work(r, z)
            if r == count - 1:
                send_off(1, z)
    for r in range(count):
        ebuf[1, g, r : r + 1] = jnp.sum(eacc[r], axis=0, keepdims=True)

    def received(c, z):
        along(1, lambda: ship(c, z, 1).wait_recv())
        along(-1, lambda: ship(c, z, 0).wait_recv())

    for z in range(planes):
        received(0, z)
    along(1, lambda: tell(1).wait_recv())
    along(-1, lambda: tell(0).wait_recv())

    def share(dt, source, there):
        return pltpu.make_async_remote_copy(
            src_ref=ebuf.at[1, source],
            dst_ref=ebuf.at[1 - dt, source],
            send_sem=esend.at[1 - dt, there],
            recv_sem=erecv.at[1 - dt, source],
            device_id=peer(dt, there),
            device_id_type=MESH,
        )

    def spread(dt, action):
        def all_of():
            for d in range(1 if dt == 0 else 0, n):
                action(lax.rem(g + d, n))

        along(dt, all_of)

    for dt in (0, 1, -1):
        spread(dt, lambda there, dt=dt: share(dt, g, there).start())
    for z in range(1, last):
        received(1, z)
    for r in range(count):
        for side in (0, 1):
            halo(x, r, side).wait_send()
    along(1, lambda: tell(0).wait_send())
    along(-1, lambda: tell(1).wait_send())
    for z in range(planes):
        for c in (0, 1):
            along(1, lambda: ship(c, z, 0).wait_send())
            along(-1, lambda: ship(c, z, 1).wait_send())
    for z in (0, last):
        received(1, z)
    for dt in (0, 1, -1):
        spread(dt, lambda there, dt=dt: share(dt, g, there).wait_send())
    for dt in (0, 1, -1):
        spread(-dt, lambda there, dt=dt: share(dt, there, there).wait_recv())


def finish_kernel(
    dims,
    evened,
    rbuf,
    trecv,
    ebuf,
    out_hbm,
    eout_ref,
    stage,
    out_sem,
):
    count, planes, rows, width, n, m = dims
    k = rows // 2
    g = lax.axis_index("gz")
    t = lax.axis_index("temp")
    below, above = (t > 0).astype(jnp.int32), (t < m - 1).astype(jnp.int32)

    def number(side, row):
        return trecv[side, row : row + 1]

    def own_order(r):
        return number(2, r)

    def own_bit(r):
        return number(2, count + r)

    def mask(value, size):
        return jnp.broadcast_to(value, (size, width)) > 0.5

    def plan(r):
        if r == 0:
            met = jnp.full((1, width), below, jnp.int32) != 0
            return rbuf.at[0], jnp.where(met, number(0, 1), 0.0), jnp.where(met, number(0, 0), 0.0)
        if r == count - 1:
            met = jnp.full((1, width), above, jnp.int32) != 0
            return rbuf.at[1], jnp.where(met, own_bit(r), 0.0), jnp.where(met, number(1, 0), 0.0)
        other = r + 1 if r % 2 else r - 1
        return evened.at[other], own_bit(min(r, other)), own_order(other)

    lane = lax.broadcasted_iota(jnp.int32, (k, width), 1)
    plans = [plan(r) for r in range(count)]
    orders = [
        jnp.where(take > 0.5, order, own_order(r)).astype(jnp.int32)
        for r, (_, take, order) in enumerate(plans)
    ]
    copies = []
    for z in range(planes):
        for r in range(count):
            other, take, _ = plans[r]
            taking = mask(take, k)
            e = ((lane + (jnp.broadcast_to(orders[r], (k, width)) + (g * planes + z))) & 1) != 0
            for d in range(3):
                first, second = [
                    jnp.where(taking, other[c, z, d], evened[r, c, z, d]) for c in (0, 1)
                ]
                stage[r, d, z, pl.ds(0, k, stride=2), :] = jnp.where(e, second, first)
                stage[r, d, z, pl.ds(1, k, stride=2), :] = jnp.where(e, first, second)
            copy = pltpu.make_async_copy(
                stage.at[r, :, z], out_hbm.at[r, :, z], out_sem.at[r, z]
            )
            copy.start()
            copies.append(copy)

    sites = float(width * rows * planes * n)

    def total(slot, r):
        summed = ebuf[slot, 0, r : r + 1]
        for j in range(1, n):
            summed = summed + ebuf[slot, j, r : r + 1]
        return jnp.broadcast_to(jnp.sum(-summed, axis=1, keepdims=True) / sites, (1, width))

    energy = []
    for r in range(0, count, 2):
        taking = own_bit(r) > 0.5
        low, top = total(1, r), total(1, r + 1)
        energy += [jnp.where(taking, top, low), jnp.where(taking, low, top)]
    for r in range(count):
        other, take, _ = plans[r]
        if r == 0:
            swapped = number(0, 2) > 0.5
            partner = jnp.where(swapped, total(0, count - 2), total(0, count - 1))
        elif r == count - 1:
            swapped = number(1, 2) > 0.5
            partner = jnp.where(swapped, total(2, 1), total(2, 0))
        else:
            partner = energy[r + 1 if r % 2 else r - 1]
        eout_ref[r] = jnp.max(jnp.where(take > 0.5, partner, energy[r]))
    for copy in copies:
        copy.wait()


def on_device(n, m, spin, coup, beta, order, level, height, angle, bits):
    count, _, planes, rows, width = spin.shape
    k = rows // 2
    f32 = jnp.float32
    hbm = pl.BlockSpec(memory_space=pltpu.HBM)
    smem = pl.BlockSpec(memory_space=pltpu.SMEM)
    vmem = pl.BlockSpec(memory_space=pltpu.VMEM)
    dma = pltpu.SemaphoreType.DMA
    bonds = pltpu.VMEM((2, count, planes, k, width), f32)
    dims = (count, planes, rows, width, n, m)
    handed = pl.pallas_call(
        functools.partial(sweep_kernel, dims),
        out_shape=(
            pltpu.VMEM((count, 2, planes, 3, k, width), f32),
            pltpu.VMEM((2, 2, planes, 3, k, width), f32),
            pltpu.VMEM((3, max(8, 2 * count), width), f32),
            pltpu.VMEM((3, n, count, width), f32),
        ),
        in_specs=[hbm, hbm, smem, smem, hbm, hbm, hbm, smem],
        out_specs=(vmem,) * 4,
        scratch_shapes=[
            pltpu.VMEM(spin.shape, f32),
            pltpu.VMEM(coup.shape, f32),
            pltpu.VMEM(level.shape, f32),
            pltpu.VMEM(level.shape, f32),
            pltpu.VMEM(level.shape, f32),
            pltpu.VMEM((2, count, 3, k, width), f32),
            pltpu.VMEM((2, count, 3, planes + 2, k + 2 * PAD, width), f32),
            bonds,
            bonds,
            pltpu.VMEM((count, planes, k, width), f32),
            bonds,
            bonds,
            bonds,
            bonds,
            pltpu.VMEM((2, count, 3, planes, k, width), f32),
            pltpu.VMEM((count, 8, width), f32),
            pltpu.VMEM((2, max(8, 2 * count), width), f32),
            dma((9,)),
            dma((HALVES, count, 2)),
            dma((HALVES, count, 2)),
            dma((3, n)),
            dma((3, n)),
            dma((2,)),
            dma((2,)),
            dma((2, planes, 2)),
            dma((2, planes, 2)),
            pltpu.SemaphoreType.REGULAR,
        ],
        compiler_params=pltpu.CompilerParams(
            collective_id=0, has_side_effects=True, vmem_limit_bytes=58 * 1024 * 1024
        ),
    )(spin, coup, beta, order, level, height, angle, bits)
    return pl.pallas_call(
        functools.partial(finish_kernel, dims),
        out_shape=(
            jax.ShapeDtypeStruct(spin.shape, f32),
            jax.ShapeDtypeStruct((count,), f32),
        ),
        in_specs=[vmem] * 4,
        out_specs=(hbm, smem),
        scratch_shapes=[pltpu.VMEM(spin.shape, f32), dma((count, planes))],
        compiler_params=pltpu.CompilerParams(vmem_limit_bytes=16 * 1024 * 1024),
    )(*handed)


def solution(mesh):
    n, m = mesh.shape["gz"], mesh.shape["temp"]
    return jax.shard_map(
        functools.partial(on_device, n, m),
        mesh=mesh,
        in_specs=(
            P(("group", "temp"), None, "gz", None, None),
            P(None, ("group", "gz"), None, None),
            P(("group", "temp")),
            P(("group", "temp")),
            P(("group", "temp"), "gz", None, None),
            P(("group", "temp"), "gz", None, None),
            P(("group", "temp"), "gz", None, None),
            P(("group", "temp")),
        ),
        out_specs=(P(("group", "temp"), None, "gz", None, None), P(("group", "temp"))),
        check_vma=False,
    )
```

time: 71.4 us -> 66.8 us (0.936)
  local copies, waits for them, and re-layouts: 3.22 us -> 0 us
  Pallas kernels: 67.4 us -> 66 us
    unnamed x4 -> x0, local copies, waits for them, and re-layouts: 3.22 us -> none
    pallas_call x1 -> x2, Pallas kernels: 67.4 us -> 66 us  [the longest x1 64.1 us: on_device(): pl.pallas_call(functools.partial(sweep_kernel, dims), out_shape=(pltpu.VM...]
where the time goes in v1:
time: 66.8 us; the launch traced here: 66.6 us
  Pallas kernels  66 us (99%)
    pallas_call x1, Pallas kernels, on_device(): pl.pallas_call(functools.partial(sweep_kernel, dims), out_shape=(pltpu.VM...  64.1 us
    pallas_call x1, Pallas kernels, on_device(): pl.pallas_call(functools.partial(finish_kernel, dims), out_shape=(jax.Sha...  1.82 us

profile of v1, /device:TPU:1, one launch (start us, length us, event | category | flops | bytes accessed | tf_op | source)
XLA Modules:
  0.0 66.6 jit_solution(5456047640981449280)
XLA Ops:
  0.6 64.1 %shard_map.95 = (f32[2,2,4,3,64,128]{5,4,3,2,1,0:T(8,128)S(1)}, f32[2,2,4,3,64,128]{5,4,3,2,1,0:T(8,128)S(1)}, f32[3,8,128]{2,1,0:T(8,128)S(1)}, f32[3,4,2,128]{3,2,1,0:T(2,128)S(1)}) custom-call(f32[2,3,4,128,128]{4,3,2,1,0:T(8,128)} %spin_hbm.1, f32[3,4,128,128]{3,2,1,0:T(8,128)} %coup_hbm.1, f32[2]{0:T(128)} %beta_ref.1, s32[2]{0:T(128)} %order_ref.1, ...), custom_call_target="tpu_custom_call" | custom-call | tf_op jit(solution)/shard_map/pallas_call | solution.py:584
  64.8 1.8 %shard_map.96 = (f32[2,3,4,128,128]{4,3,2,1,0:T(8,128)}, f32[2]{0:T(128)}) custom-call(f32[2,2,4,3,64,128]{5,4,3,2,1,0:T(8,128)S(1)} %get-tuple-element.6.evened, f32[2,2,4,3,64,128]{5,4,3,2,1,0:T(8,128)S(1)} %get-tuple-element.7.rbuf, f32[3,8,128]{2,1,0:T(8,128)S(1)} %get-tuple-element.8.trecv, f32[3,4,2,128]{3,2,1,0:T(2,128)S(1)} %get-tuple-element.9.ebuf), custom_call_target="tpu_custom_call" | custom-call | tf_op jit(solution)/shard_map/pallas_call | solution.py:627

commit v2 on v1

--- a/solution.py
+++ b/solution.py
@@ -63,12 +63,12 @@
     dims,
     spin_hbm,
     coup_hbm,
-    beta_ref,
-    order_ref,
+    beta_hbm,
+    order_hbm,
     level_hbm,
     height_hbm,
     angle_hbm,
-    bits_ref,
+    bits_hbm,
     evened,
     rbuf,
     trecv,
@@ -90,6 +90,9 @@
     ut,
     eacc,
     tsend,
+    beta_ref,
+    order_ref,
+    bits_ref,
     in_sem,
     hsend,
     hrecv,
@@ -127,6 +130,9 @@
                 (level_hbm, level_in),
                 (height_hbm, height_in),
                 (angle_hbm, angle_in),
+                (order_hbm, order_ref),
+                (bits_hbm, bits_ref),
+                (beta_hbm, beta_ref),
             )
         )
     ]
@@ -139,6 +145,10 @@
             action()
         else:
             pl.when(has_below if dt < 0 else has_above)(action)
+
+    scalars = loads[9:]
+    for load in loads[:3] + scalars:
+        load.start()
 
     barrier = pltpu.get_barrier_semaphore()
 
@@ -165,9 +175,6 @@
 
             along(dt, greet_all)
         expected = n - 1 + n * sides
-
-    for load in loads:
-        load.start()
 
     def parity(r, z, size):
         lane = lax.broadcasted_iota(jnp.int32, (size, width), 1)
@@ -193,14 +200,23 @@
             put_spin(0, r, d, z, 0, jnp.where(e, odd, even))
             put_spin(1, r, d, z, 0, jnp.where(e, even, odd))
 
-    def halo(x, r, side):
+    middle = k // chunk // 2 * chunk
+
+    def parts(x, r):
+        split = x == HALVES - 1 and r == count - 1 and middle > 0
+        return [(0, middle), (middle, k)] if split else [(0, k)]
+
+    def halo(x, r, side, part=0):
         c = 1 - x % 2
-        plain = sp.at[c, r, :, 1, pl.ds(PAD, k), :]
+        start, stop = parts(x, r)[part]
+        size = stop - start
+        plain = sp.at[c, r, :, 1, pl.ds(PAD + start, size), :]
+        above = planes + 1 if side == 0 else 0
         return pltpu.make_async_remote_copy(
-            src_ref=plain if side == 0 else lifted.at[c, r],
-            dst_ref=sp.at[c, r, :, planes + 1 if side == 0 else 0, pl.ds(PAD, k), :],
-            send_sem=hsend.at[x, r, side],
-            recv_sem=hrecv.at[x, r, side],
+            src_ref=plain if side == 0 else lifted.at[c, r, :, pl.ds(start, size), :],
+            dst_ref=sp.at[c, r, :, above, pl.ds(PAD + start, size), :],
+            send_sem=hsend.at[x + part, r, side],
+            recv_sem=hrecv.at[x + part, r, side],
             device_id={"gz": down if side == 0 else up},
             device_id_type=MESH,
         )
@@ -213,9 +229,22 @@
         if planes > 2:
             lax.fori_loop(1, last, lambda z, carry: (action(r, z), carry)[1], 0)
 
-    for load in loads[:3]:
+    def ready():
+        pl.semaphore_wait(barrier, expected)
+
+    if near:
+
+        @pl.when(g == n - 1)
+        def _():
+            ready()
+            pl.semaphore_signal(wrap_sem, inc=1, device_id={"gz": up}, device_id_type=MESH)
+
+    for load in loads[:3] + scalars:
         load.wait()
-    for r in range(count):
+    for load in loads[3:9]:
+        load.start()
+
+    def pack_edges(r):
         e = parity(r, last, k)
         even, odd = halves(coup_in, (2, last), 0, k)
         zu[0, r, last] = jnp.where(e, odd, even)
@@ -232,6 +261,22 @@
     def wide(value):
         return jnp.full((1, width), value, jnp.int32).astype(jnp.float32)
 
+    for r in range(count):
+        pack_edges(r)
+        if r == 0:
+            if near:
+                pl.when(g < n - 1)(ready)
+            else:
+                ready()
+        halo(0, r, 1).start()
+        if r == 0 and near:
+
+            @pl.when(g == 0)
+            def _():
+                pl.semaphore_wait(wrap_sem, 1)
+
+        halo(0, r, 0).start()
+
     tsend[0, 0:1] = wide(slot_order(count - 1))
     tsend[0, 1:2] = wide(bits_ref[count - 1])
     tsend[0, 2:3] = wide(bits_ref[count - 2])
@@ -241,23 +286,6 @@
     for r in range(count):
         trecv[2, r : r + 1] = wide(slot_order(r))
         trecv[2, count + r : count + r + 1] = wide(bits_ref[r])
-
-    pl.semaphore_wait(barrier, expected)
-    if near:
-
-        @pl.when(g == n - 1)
-        def _():
-            pl.semaphore_signal(wrap_sem, inc=1, device_id={"gz": up}, device_id_type=MESH)
-
-    for r in range(count):
-        halo(0, r, 1).start()
-        if r == 0 and near:
-
-            @pl.when(g == 0)
-            def _():
-                pl.semaphore_wait(wrap_sem, 1)
-
-        halo(0, r, 0).start()
 
     def tell(side):
         return pltpu.make_async_remote_copy(
@@ -337,8 +365,8 @@
                 if lifting:
                     lift(c, r, d, start, value)
 
-    def heat(c, r, z, lifting=False):
-        for start in range(0, k, chunk):
+    def heat(c, r, z, lifting=False, rows_of=(0, k)):
+        for start in range(*rows_of, chunk):
             part = pl.ds(start, chunk)
             pulled = pull(c, r, z, start)
             trial = [ut[c, r, d, z, part, :] for d in range(3)]
@@ -383,38 +411,52 @@
             for side, z in ((0, 0), (1, last)):
                 take_halo(x, r, side)
                 work(r, z, lifting=side == 1)
-                halo(x + 1, r, side).start()
+                if len(parts(x + 1, r)) == 1:
+                    halo(x + 1, r, side).start()
+            if len(parts(x + 1, r)) > 1:
+                for part in (0, 1):
+                    for side in (0, 1):
+                        halo(x + 1, r, side, part).start()
             inner(r, work)
             if x == 0 and r == 0:
-                for load in loads[6:]:
+                for load in loads[6:9]:
                     load.wait()
             for z in range(planes):
                 if z % relaxing == x:
                     pack_heat(r, z)
 
-    def settle(c, z):
+    def settle(c, z, start, stop):
+        size = stop - start
+        part, packed = pl.ds(start, size), pl.ds(PAD + start, size)
         for r in range(0, count, 2):
-            taking = flag(bits_ref, r, k, width)
+            taking = flag(bits_ref, r, size, width)
             for d in range(3):
-                low = sp[c, r, d, z + 1, pl.ds(PAD, k), :]
-                top = sp[c, r + 1, d, z + 1, pl.ds(PAD, k), :]
-                evened[r, c, z, d] = jnp.where(taking, top, low)
-                evened[r + 1, c, z, d] = jnp.where(taking, low, top)
-
-    def ship(c, z, side):
+                low = sp[c, r, d, z + 1, packed, :]
+                top = sp[c, r + 1, d, z + 1, packed, :]
+                evened[r, c, z, d, part, :] = jnp.where(taking, top, low)
+                evened[r + 1, c, z, d, part, :] = jnp.where(taking, low, top)
+
+    final = parts(HALVES - 1, count - 1)
+
+    def pieces(c, z):
+        return final if c == 1 and z in (0, last) else [(0, k)]
+
+    def ship(c, z, side, part):
+        start, stop = pieces(c, z)[part]
+        rows_of = pl.ds(start, stop - start)
         return pltpu.make_async_remote_copy(
-            src_ref=evened.at[count - 1 if side == 0 else 0, c, z],
-            dst_ref=rbuf.at[side, c, z],
-            send_sem=xsend.at[c, z, side],
-            recv_sem=xrecv.at[c, z, side],
+            src_ref=evened.at[count - 1 if side == 0 else 0, c, z, :, rows_of, :],
+            dst_ref=rbuf.at[side, c, z, :, rows_of, :],
+            send_sem=xsend.at[c, z, side, part],
+            recv_sem=xrecv.at[c, z, side, part],
             device_id={"temp": t + 1 if side == 0 else t - 1},
             device_id_type=MESH,
         )
 
-    def send_off(c, z):
-        settle(c, z)
-        along(1, lambda: ship(c, z, 0).start())
-        along(-1, lambda: ship(c, z, 1).start())
+    def send_off(c, z, part=0):
+        settle(c, z, *pieces(c, z)[part])
+        along(1, lambda: ship(c, z, 0, part).start())
+        along(-1, lambda: ship(c, z, 1, part).start())
 
     x = HALVES - 1
     work = functools.partial(heat, 1)
@@ -425,17 +467,21 @@
     for z in range(1, last):
         send_off(1, z)
     for r in range(count):
-        for side, z in ((0, 0), (1, last)):
-            take_halo(x, r, side)
-            work(r, z)
-            if r == count - 1:
-                send_off(1, z)
+        for part, rows_of in enumerate(parts(x, r)):
+            for side, z in ((0, 0), (1, last)):
+                halo(x, r, 1 - side, part).wait_recv()
+                if part == 0:
+                    halo(x - 1, r, side).wait_send()
+                work(r, z, rows_of=rows_of)
+                if r == count - 1:
+                    send_off(1, z, part)
     for r in range(count):
         ebuf[1, g, r : r + 1] = jnp.sum(eacc[r], axis=0, keepdims=True)
 
     def received(c, z):
-        along(1, lambda: ship(c, z, 1).wait_recv())
-        along(-1, lambda: ship(c, z, 0).wait_recv())
+        for part in range(len(pieces(c, z))):
+            along(1, lambda: ship(c, z, 1, part).wait_recv())
+            along(-1, lambda: ship(c, z, 0, part).wait_recv())
 
     for z in range(planes):
         received(0, z)
@@ -465,13 +511,15 @@
         received(1, z)
     for r in range(count):
         for side in (0, 1):
-            halo(x, r, side).wait_send()
+            for part in range(len(parts(x, r))):
+                halo(x, r, side, part).wait_send()
     along(1, lambda: tell(0).wait_send())
     along(-1, lambda: tell(1).wait_send())
     for z in range(planes):
         for c in (0, 1):
-            along(1, lambda: ship(c, z, 0).wait_send())
-            along(-1, lambda: ship(c, z, 1).wait_send())
+            for part in range(len(pieces(c, z))):
+                along(1, lambda: ship(c, z, 0, part).wait_send())
+                along(-1, lambda: ship(c, z, 1, part).wait_send())
     for z in (0, last):
         received(1, z)
     for dt in (0, 1, -1):
@@ -487,9 +535,11 @@
     trecv,
     ebuf,
     out_hbm,
+    eout_hbm,
+    stage,
     eout_ref,
-    stage,
     out_sem,
+    eout_sem,
 ):
     count, planes, rows, width, n, m = dims
     k = rows // 2
@@ -525,6 +575,32 @@
         jnp.where(take > 0.5, order, own_order(r)).astype(jnp.int32)
         for r, (_, take, order) in enumerate(plans)
     ]
+    sites = float(width * rows * planes * n)
+
+    def total(slot, r):
+        summed = ebuf[slot, 0, r : r + 1]
+        for j in range(1, n):
+            summed = summed + ebuf[slot, j, r : r + 1]
+        return jnp.broadcast_to(jnp.sum(-summed, axis=1, keepdims=True) / sites, (1, width))
+
+    energy = []
+    for r in range(0, count, 2):
+        taking = own_bit(r) > 0.5
+        low, top = total(1, r), total(1, r + 1)
+        energy += [jnp.where(taking, top, low), jnp.where(taking, low, top)]
+    for r in range(count):
+        other, take, _ = plans[r]
+        if r == 0:
+            swapped = number(0, 2) > 0.5
+            partner = jnp.where(swapped, total(0, count - 2), total(0, count - 1))
+        elif r == count - 1:
+            swapped = number(1, 2) > 0.5
+            partner = jnp.where(swapped, total(2, 1), total(2, 0))
+        else:
+            partner = energy[r + 1 if r % 2 else r - 1]
+        eout_ref[r] = jnp.max(jnp.where(take > 0.5, partner, energy[r]))
+    told = pltpu.make_async_copy(eout_ref, eout_hbm, eout_sem)
+    told.start()
     copies = []
     for z in range(planes):
         for r in range(count):
@@ -542,31 +618,7 @@
             )
             copy.start()
             copies.append(copy)
-
-    sites = float(width * rows * planes * n)
-
-    def total(slot, r):
-        summed = ebuf[slot, 0, r : r + 1]
-        for j in range(1, n):
-            summed = summed + ebuf[slot, j, r : r + 1]
-        return jnp.broadcast_to(jnp.sum(-summed, axis=1, keepdims=True) / sites, (1, width))
-
-    energy = []
-    for r in range(0, count, 2):
-        taking = own_bit(r) > 0.5
-        low, top = total(1, r), total(1, r + 1)
-        energy += [jnp.where(taking, top, low), jnp.where(taking, low, top)]
-    for r in range(count):
-        other, take, _ = plans[r]
-        if r == 0:
-            swapped = number(0, 2) > 0.5
-            partner = jnp.where(swapped, total(0, count - 2), total(0, count - 1))
-        elif r == count - 1:
-            swapped = number(1, 2) > 0.5
-            partner = jnp.where(swapped, total(2, 1), total(2, 0))
-        else:
-            partner = energy[r + 1 if r % 2 else r - 1]
-        eout_ref[r] = jnp.max(jnp.where(take > 0.5, partner, energy[r]))
+    told.wait()
     for copy in copies:
         copy.wait()
 
@@ -576,7 +628,6 @@
     k = rows // 2
     f32 = jnp.float32
     hbm = pl.BlockSpec(memory_space=pltpu.HBM)
-    smem = pl.BlockSpec(memory_space=pltpu.SMEM)
     vmem = pl.BlockSpec(memory_space=pltpu.VMEM)
     dma = pltpu.SemaphoreType.DMA
     bonds = pltpu.VMEM((2, count, planes, k, width), f32)
@@ -589,7 +640,7 @@
             pltpu.VMEM((3, max(8, 2 * count), width), f32),
             pltpu.VMEM((3, n, count, width), f32),
         ),
-        in_specs=[hbm, hbm, smem, smem, hbm, hbm, hbm, smem],
+        in_specs=[hbm] * 8,
         out_specs=(vmem,) * 4,
         scratch_shapes=[
             pltpu.VMEM(spin.shape, f32),
@@ -609,15 +660,18 @@
             pltpu.VMEM((2, count, 3, planes, k, width), f32),
             pltpu.VMEM((count, 8, width), f32),
             pltpu.VMEM((2, max(8, 2 * count), width), f32),
-            dma((9,)),
-            dma((HALVES, count, 2)),
-            dma((HALVES, count, 2)),
+            pltpu.SMEM((count,), f32),
+            pltpu.SMEM((count,), jnp.int32),
+            pltpu.SMEM((count,), jnp.int32),
+            dma((12,)),
+            dma((HALVES + 1, count, 2)),
+            dma((HALVES + 1, count, 2)),
             dma((3, n)),
             dma((3, n)),
             dma((2,)),
             dma((2,)),
-            dma((2, planes, 2)),
-            dma((2, planes, 2)),
+            dma((2, planes, 2, 2)),
+            dma((2, planes, 2, 2)),
             pltpu.SemaphoreType.REGULAR,
         ],
         compiler_params=pltpu.CompilerParams(
@@ -631,8 +685,13 @@
             jax.ShapeDtypeStruct((count,), f32),
         ),
         in_specs=[vmem] * 4,
-        out_specs=(hbm, smem),
-        scratch_shapes=[pltpu.VMEM(spin.shape, f32), dma((count, planes))],
+        out_specs=(hbm, hbm),
+        scratch_shapes=[
+            pltpu.VMEM(spin.shape, f32),
+            pltpu.SMEM((count,), f32),
+            dma((count, planes)),
+            dma(()),
+        ],
         compiler_params=pltpu.CompilerParams(vmem_limit_bytes=16 * 1024 * 1024),
     )(*handed)
 

time: 66.8 us -> 65.4 us (0.979)
  Pallas kernels: 66 us -> 64.6 us
    pallas_call x1, Pallas kernels: 64.1 us -> 63.3 us  [on_device(): pl.pallas_call(functools.partial(sweep_kernel, dims), out_shape=(pltpu.VM...]
where the time goes in v2:
time: 65.4 us; the launch traced here: 65.2 us
  Pallas kernels  64.6 us (99%)
    pallas_call x1, Pallas kernels, on_device(): pl.pallas_call(functools.partial(sweep_kernel, dims), out_shape=(pltpu.VM...  63.3 us
    pallas_call x1, Pallas kernels, on_device(): pl.pallas_call(functools.partial(finish_kernel, dims), out_shape=(jax.Sha...  1.31 us

profile of v2, /device:TPU:1, one launch (start us, length us, event | category | flops | bytes accessed | tf_op | source)
XLA Modules:
  0.0 65.2 jit_solution(11529876075564547534)
XLA Ops:
  0.6 63.3 %shard_map.95 = (f32[2,2,4,3,64,128]{5,4,3,2,1,0:T(8,128)S(1)}, f32[2,2,4,3,64,128]{5,4,3,2,1,0:T(8,128)S(1)}, f32[3,8,128]{2,1,0:T(8,128)S(1)}, f32[3,4,2,128]{3,2,1,0:T(2,128)S(1)}) custom-call(f32[2,3,4,128,128]{4,3,2,1,0:T(8,128)} %spin_hbm.1, f32[3,4,128,128]{3,2,1,0:T(8,128)} %coup_hbm.1, f32[2]{0:T(128)} %beta_hbm.1, s32[2]{0:T(128)} %order_hbm.1, ...), custom_call_target="tpu_custom_call" | custom-call | tf_op jit(solution)/shard_map/pallas_call | solution.py:635
  63.9 1.3 %shard_map.96 = (f32[2,3,4,128,128]{4,3,2,1,0:T(8,128)}, f32[2]{0:T(128)}) custom-call(f32[2,2,4,3,64,128]{5,4,3,2,1,0:T(8,128)S(1)} %get-tuple-element.6.evened, f32[2,2,4,3,64,128]{5,4,3,2,1,0:T(8,128)S(1)} %get-tuple-element.7.rbuf, f32[3,8,128]{2,1,0:T(8,128)S(1)} %get-tuple-element.8.trecv, f32[3,4,2,128]{3,2,1,0:T(2,128)S(1)} %get-tuple-element.9.ebuf), custom_call_target="tpu_custom_call" | custom-call | tf_op jit(solution)/shard_map/pallas_call | solution.py:681

commit v3 on v2

--- a/solution.py
+++ b/solution.py
@@ -115,12 +115,15 @@
     near = 2 < n <= 2 * HALVES - 2
 
     loads = [
-        pltpu.make_async_copy(src, dst, in_sem.at[i])
+        pltpu.make_async_copy(src, dst, in_sem.at[i % 6])
         for i, (src, dst) in enumerate(
             (
                 (spin_hbm.at[:, :, pl.ds(0, 1)], spin_in.at[:, :, pl.ds(0, 1)]),
                 (spin_hbm.at[:, :, pl.ds(last, 1)], spin_in.at[:, :, pl.ds(last, 1)]),
                 (coup_hbm.at[2, last], coup_in.at[2, last]),
+                (order_hbm, order_ref),
+                (bits_hbm, bits_ref),
+                (beta_hbm, beta_ref),
                 (coup_hbm.at[pl.ds(0, 2)], coup_in.at[pl.ds(0, 2)]),
                 (coup_hbm.at[2, pl.ds(0, last)], coup_in.at[2, pl.ds(0, last)]),
                 (
@@ -130,9 +133,6 @@
                 (level_hbm, level_in),
                 (height_hbm, height_in),
                 (angle_hbm, angle_in),
-                (order_hbm, order_ref),
-                (bits_hbm, bits_ref),
-                (beta_hbm, beta_ref),
             )
         )
     ]
@@ -146,8 +146,7 @@
         else:
             pl.when(has_below if dt < 0 else has_above)(action)
 
-    scalars = loads[9:]
-    for load in loads[:3] + scalars:
+    for load in loads[:6]:
         load.start()
 
     barrier = pltpu.get_barrier_semaphore()
@@ -215,11 +214,15 @@
         return pltpu.make_async_remote_copy(
             src_ref=plain if side == 0 else lifted.at[c, r, :, pl.ds(start, size), :],
             dst_ref=sp.at[c, r, :, above, pl.ds(PAD + start, size), :],
-            send_sem=hsend.at[x + part, r, side],
-            recv_sem=hrecv.at[x + part, r, side],
+            send_sem=hsend.at[x % 2, r],
+            recv_sem=hrecv.at[2 if part else x % 2, r if part == 0 else 0, side],
             device_id={"gz": down if side == 0 else up},
             device_id_type=MESH,
         )
+
+    def sent(x, r):
+        both = lifted.at[:, r]
+        pltpu.make_async_copy(both, both, hsend.at[x % 2, r]).wait()
 
     def lift(c, r, d, start, value):
         part = pl.ds(start, value.shape[0])
@@ -239,9 +242,9 @@
             ready()
             pl.semaphore_signal(wrap_sem, inc=1, device_id={"gz": up}, device_id_type=MESH)
 
-    for load in loads[:3] + scalars:
+    for load in loads[:6]:
         load.wait()
-    for load in loads[3:9]:
+    for load in loads[6:]:
         load.start()
 
     def pack_edges(r):
@@ -269,13 +272,10 @@
             else:
                 ready()
         halo(0, r, 1).start()
-        if r == 0 and near:
-
-            @pl.when(g == 0)
-            def _():
-                pl.semaphore_wait(wrap_sem, 1)
-
-        halo(0, r, 0).start()
+        if near:
+            pl.when(g > 0)(lambda: halo(0, r, 0).start())
+        else:
+            halo(0, r, 0).start()
 
     tsend[0, 0:1] = wide(slot_order(count - 1))
     tsend[0, 1:2] = wide(bits_ref[count - 1])
@@ -300,7 +300,7 @@
     along(1, lambda: tell(0).start())
     along(-1, lambda: tell(1).start())
 
-    for load in loads[3:6]:
+    for load in loads[6:9]:
         load.wait()
 
     def pack_bonds(i, carry):
@@ -336,6 +336,14 @@
     for r in range(count):
         for c in (0, 1):
             zd[c, r, 0] = jnp.ones((k, width), jnp.float32)
+
+    if near:
+
+        @pl.when(g == 0)
+        def _():
+            pl.semaphore_wait(wrap_sem, 1)
+            for r in range(count):
+                halo(0, r, 0).start()
 
     def pull(c, r, z, start):
         o = 1 - c
@@ -399,31 +407,8 @@
 
     def take_halo(x, r, side):
         halo(x, r, 1 - side).wait_recv()
-        if x >= 1:
-            halo(x - 1, r, side).wait_send()
-
-    eacc[...] = jnp.zeros_like(eacc)
-    relaxing = 2 * OR_SWEEPS
-    for x in range(HALVES - 1):
-        c = x % 2
-        work = functools.partial(relax if x < relaxing else heat, c)
-        for r in range(count):
-            for side, z in ((0, 0), (1, last)):
-                take_halo(x, r, side)
-                work(r, z, lifting=side == 1)
-                if len(parts(x + 1, r)) == 1:
-                    halo(x + 1, r, side).start()
-            if len(parts(x + 1, r)) > 1:
-                for part in (0, 1):
-                    for side in (0, 1):
-                        halo(x + 1, r, side, part).start()
-            inner(r, work)
-            if x == 0 and r == 0:
-                for load in loads[6:9]:
-                    load.wait()
-            for z in range(planes):
-                if z % relaxing == x:
-                    pack_heat(r, z)
+        if x >= 1 and side == 0:
+            sent(x - 1, r)
 
     def settle(c, z, start, stop):
         size = stop - start
@@ -433,58 +418,95 @@
             for d in range(3):
                 low = sp[c, r, d, z + 1, packed, :]
                 top = sp[c, r + 1, d, z + 1, packed, :]
-                evened[r, c, z, d, part, :] = jnp.where(taking, top, low)
-                evened[r + 1, c, z, d, part, :] = jnp.where(taking, low, top)
+                evened[r, c * planes + z, d, part, :] = jnp.where(taking, top, low)
+                evened[r + 1, c * planes + z, d, part, :] = jnp.where(taking, low, top)
 
     final = parts(HALVES - 1, count - 1)
 
     def pieces(c, z):
         return final if c == 1 and z in (0, last) else [(0, k)]
 
-    def ship(c, z, side, part):
+    def ship(c, z, side, part=0, many=1):
         start, stop = pieces(c, z)[part]
         rows_of = pl.ds(start, stop - start)
+        here = pl.ds(c * planes + z, many)
+        early = c == 0 and 0 < z < last
         return pltpu.make_async_remote_copy(
-            src_ref=evened.at[count - 1 if side == 0 else 0, c, z, :, rows_of, :],
-            dst_ref=rbuf.at[side, c, z, :, rows_of, :],
-            send_sem=xsend.at[c, z, side, part],
-            recv_sem=xrecv.at[c, z, side, part],
+            src_ref=evened.at[count - 1 if side == 0 else 0, here, :, rows_of, :],
+            dst_ref=rbuf.at[side, here, :, rows_of, :],
+            send_sem=xsend.at[side],
+            recv_sem=xrecv.at[0 if early else 1, side],
             device_id={"temp": t + 1 if side == 0 else t - 1},
             device_id_type=MESH,
         )
 
+    def both_ways(action):
+        along(1, lambda: action(0))
+        along(-1, lambda: action(1))
+
     def send_off(c, z, part=0):
         settle(c, z, *pieces(c, z)[part])
-        along(1, lambda: ship(c, z, 0, part).start())
-        along(-1, lambda: ship(c, z, 1, part).start())
+        both_ways(lambda side: ship(c, z, side, part).start())
+
+    def send_inner(c):
+        for z in range(1, last):
+            settle(c, z, 0, k)
+        if planes > 2:
+            both_ways(lambda side: ship(c, 1, side, many=planes - 2).start())
+
+    def whole(side, size, sem):
+        ref = rbuf.at[side, pl.ds(0, size)]
+        pltpu.make_async_copy(ref, ref, sem).wait()
+
+    def arrived(early):
+        size = planes - 2 if early else planes + 2
+        if size:
+            both_ways(lambda side: whole(1 - side, size, xrecv.at[0 if early else 1, 1 - side]))
+
+    def work(x):
+        return functools.partial(relax if x < relaxing else heat, x % 2)
+
+    eacc[...] = jnp.zeros_like(eacc)
+    relaxing = 2 * OR_SWEEPS
+    for r in range(count):
+        inner(r, work(0))
+    for load in loads[9:]:
+        load.wait()
+    for x in range(HALVES - 1):
+        for r in range(count):
+            for side, z in ((0, 0), (1, last)):
+                take_halo(x, r, side)
+                work(x)(r, z, lifting=side == 1)
+                if len(parts(x + 1, r)) == 1:
+                    halo(x + 1, r, side).start()
+            if len(parts(x + 1, r)) > 1:
+                for part in (0, 1):
+                    for side in (0, 1):
+                        halo(x + 1, r, side, part).start()
+            if r == count - 1 and x == relaxing:
+                for z in (0, last):
+                    send_off(0, z)
+            for z in range(planes):
+                if z % relaxing == x:
+                    pack_heat(r, z)
+            inner(r, work(x + 1))
+        if x >= relaxing - 1:
+            send_inner(x + 1 - relaxing)
 
     x = HALVES - 1
-    work = functools.partial(heat, 1)
-    for z in range(planes):
-        send_off(0, z)
-    for r in range(count):
-        inner(r, work)
-    for z in range(1, last):
-        send_off(1, z)
     for r in range(count):
         for part, rows_of in enumerate(parts(x, r)):
             for side, z in ((0, 0), (1, last)):
                 halo(x, r, 1 - side, part).wait_recv()
-                if part == 0:
-                    halo(x - 1, r, side).wait_send()
-                work(r, z, rows_of=rows_of)
+                if part == 0 and side == 0:
+                    sent(x - 1, r)
+                work(x)(r, z, rows_of=rows_of)
                 if r == count - 1:
                     send_off(1, z, part)
     for r in range(count):
         ebuf[1, g, r : r + 1] = jnp.sum(eacc[r], axis=0, keepdims=True)
 
-    def received(c, z):
-        for part in range(len(pieces(c, z))):
-            along(1, lambda: ship(c, z, 1, part).wait_recv())
-            along(-1, lambda: ship(c, z, 0, part).wait_recv())
-
-    for z in range(planes):
-        received(0, z)
+    arrived(True)
     along(1, lambda: tell(1).wait_recv())
     along(-1, lambda: tell(0).wait_recv())
 
@@ -492,40 +514,31 @@
         return pltpu.make_async_remote_copy(
             src_ref=ebuf.at[1, source],
             dst_ref=ebuf.at[1 - dt, source],
-            send_sem=esend.at[1 - dt, there],
-            recv_sem=erecv.at[1 - dt, source],
+            send_sem=esend.at[1 - dt],
+            recv_sem=erecv.at[1 - dt],
             device_id=peer(dt, there),
             device_id_type=MESH,
         )
 
-    def spread(dt, action):
-        def all_of():
-            for d in range(1 if dt == 0 else 0, n):
-                action(lax.rem(g + d, n))
-
-        along(dt, all_of)
+    def spread(dt):
+        for d in range(1 if dt == 0 else 0, n):
+            share(dt, g, lax.rem(g + d, n)).start()
+
+    def shares(dt, sem):
+        ref = ebuf.at[1, pl.ds(0, n - 1 if dt == 0 else n)]
+        pltpu.make_async_copy(ref, ref, sem).wait()
 
     for dt in (0, 1, -1):
-        spread(dt, lambda there, dt=dt: share(dt, g, there).start())
-    for z in range(1, last):
-        received(1, z)
-    for r in range(count):
-        for side in (0, 1):
-            for part in range(len(parts(x, r))):
-                halo(x, r, side, part).wait_send()
+        along(dt, lambda dt=dt: spread(dt))
+    for r in range(count):
+        sent(x, r)
     along(1, lambda: tell(0).wait_send())
     along(-1, lambda: tell(1).wait_send())
-    for z in range(planes):
-        for c in (0, 1):
-            for part in range(len(pieces(c, z))):
-                along(1, lambda: ship(c, z, 0, part).wait_send())
-                along(-1, lambda: ship(c, z, 1, part).wait_send())
-    for z in (0, last):
-        received(1, z)
+    both_ways(lambda side: whole(side, 2 * planes, xsend.at[side]))
+    arrived(False)
     for dt in (0, 1, -1):
-        spread(dt, lambda there, dt=dt: share(dt, g, there).wait_send())
-    for dt in (0, 1, -1):
-        spread(-dt, lambda there, dt=dt: share(dt, there, there).wait_recv())
+        along(dt, lambda dt=dt: shares(dt, esend.at[1 - dt]))
+        along(dt, lambda dt=dt: shares(dt, erecv.at[1 + dt]))
 
 
 def finish_kernel(
@@ -601,7 +614,6 @@
         eout_ref[r] = jnp.max(jnp.where(take > 0.5, partner, energy[r]))
     told = pltpu.make_async_copy(eout_ref, eout_hbm, eout_sem)
     told.start()
-    copies = []
     for z in range(planes):
         for r in range(count):
             other, take, _ = plans[r]
@@ -609,18 +621,16 @@
             e = ((lane + (jnp.broadcast_to(orders[r], (k, width)) + (g * planes + z))) & 1) != 0
             for d in range(3):
                 first, second = [
-                    jnp.where(taking, other[c, z, d], evened[r, c, z, d]) for c in (0, 1)
+                    jnp.where(taking, other[i, d], evened[r, i, d]) for i in (z, planes + z)
                 ]
                 stage[r, d, z, pl.ds(0, k, stride=2), :] = jnp.where(e, second, first)
                 stage[r, d, z, pl.ds(1, k, stride=2), :] = jnp.where(e, first, second)
             copy = pltpu.make_async_copy(
-                stage.at[r, :, z], out_hbm.at[r, :, z], out_sem.at[r, z]
+                stage.at[r, :, z], out_hbm.at[r, :, z], out_sem
             )
             copy.start()
-            copies.append(copy)
     told.wait()
-    for copy in copies:
-        copy.wait()
+    pltpu.make_async_copy(stage, out_hbm, out_sem).wait()
 
 
 def on_device(n, m, spin, coup, beta, order, level, height, angle, bits):
@@ -635,8 +645,8 @@
     handed = pl.pallas_call(
         functools.partial(sweep_kernel, dims),
         out_shape=(
-            pltpu.VMEM((count, 2, planes, 3, k, width), f32),
-            pltpu.VMEM((2, 2, planes, 3, k, width), f32),
+            pltpu.VMEM((count, 2 * planes, 3, k, width), f32),
+            pltpu.VMEM((2, 2 * planes, 3, k, width), f32),
             pltpu.VMEM((3, max(8, 2 * count), width), f32),
             pltpu.VMEM((3, n, count, width), f32),
         ),
@@ -663,15 +673,15 @@
             pltpu.SMEM((count,), f32),
             pltpu.SMEM((count,), jnp.int32),
             pltpu.SMEM((count,), jnp.int32),
-            dma((12,)),
-            dma((HALVES + 1, count, 2)),
-            dma((HALVES + 1, count, 2)),
-            dma((3, n)),
-            dma((3, n)),
+            dma((6,)),
+            dma((2, count)),
+            dma((3, count, 2)),
+            dma((3,)),
+            dma((3,)),
             dma((2,)),
             dma((2,)),
-            dma((2, planes, 2, 2)),
-            dma((2, planes, 2, 2)),
+            dma((2,)),
+            dma((2, 2)),
             pltpu.SemaphoreType.REGULAR,
         ],
         compiler_params=pltpu.CompilerParams(
@@ -689,7 +699,7 @@
         scratch_shapes=[
             pltpu.VMEM(spin.shape, f32),
             pltpu.SMEM((count,), f32),
-            dma((count, planes)),
+            dma(()),
             dma(()),
         ],
         compiler_params=pltpu.CompilerParams(vmem_limit_bytes=16 * 1024 * 1024),

time: 65.4 us -> 63.6 us (0.972)
  Pallas kernels: 64.6 us -> 62.8 us
    pallas_call x1, Pallas kernels: 63.3 us -> 61.6 us  [on_device(): pl.pallas_call(functools.partial(sweep_kernel, dims), out_shape=(pltpu.VM...]
where the time goes in v3:
time: 63.6 us; the launch traced here: 63.5 us
  Pallas kernels  62.8 us (99%)
  between operations  0.64 us (1%)
    pallas_call x1, Pallas kernels, on_device(): pl.pallas_call(functools.partial(sweep_kernel, dims), out_shape=(pltpu.VM...  61.6 us

profile of v3, /device:TPU:1, one launch (start us, length us, event | category | flops | bytes accessed | tf_op | source)
XLA Modules:
  0.0 63.5 jit_solution(4841859636681733943)
XLA Ops:
  0.6 61.6 %shard_map.95 = (f32[2,8,3,64,128]{4,3,2,1,0:T(8,128)S(1)}, f32[2,8,3,64,128]{4,3,2,1,0:T(8,128)S(1)}, f32[3,8,128]{2,1,0:T(8,128)S(1)}, f32[3,4,2,128]{3,2,1,0:T(2,128)S(1)}) custom-call(f32[2,3,4,128,128]{4,3,2,1,0:T(8,128)} %spin_hbm.1, f32[3,4,128,128]{3,2,1,0:T(8,128)} %coup_hbm.1, f32[2]{0:T(128)} %beta_hbm.1, s32[2]{0:T(128)} %order_hbm.1, ...), custom_call_target="tpu_custom_call" | custom-call | tf_op jit(solution)/shard_map/pallas_call | solution.py:645
  62.2 1.2 %shard_map.96 = (f32[2,3,4,128,128]{4,3,2,1,0:T(8,128)}, f32[2]{0:T(128)}) custom-call(f32[2,8,3,64,128]{4,3,2,1,0:T(8,128)S(1)} %get-tuple-element.6.evened, f32[2,8,3,64,128]{4,3,2,1,0:T(8,128)S(1)} %get-tuple-element.7.rbuf, f32[3,8,128]{2,1,0:T(8,128)S(1)} %get-tuple-element.8.trecv, f32[3,4,2,128]{3,2,1,0:T(2,128)S(1)} %get-tuple-element.9.ebuf), custom_call_target="tpu_custom_call" | custom-call | tf_op jit(solution)/shard_map/pallas_call | solution.py:691

commit v4 on v3

--- a/solution.py
+++ b/solution.py
@@ -114,14 +114,18 @@
     has_below, has_above = t > 0, t < m - 1
     near = 2 < n <= 2 * HALVES - 2
 
+    first = 2 * count + 4
     loads = [
-        pltpu.make_async_copy(src, dst, in_sem.at[i % 6])
+        pltpu.make_async_copy(src, dst, in_sem.at[i % first])
         for i, (src, dst) in enumerate(
             (
-                (spin_hbm.at[:, :, pl.ds(0, 1)], spin_in.at[:, :, pl.ds(0, 1)]),
-                (spin_hbm.at[:, :, pl.ds(last, 1)], spin_in.at[:, :, pl.ds(last, 1)]),
+                (order_hbm, order_ref),
                 (coup_hbm.at[2, last], coup_in.at[2, last]),
-                (order_hbm, order_ref),
+                *(
+                    (spin_hbm.at[r, :, z], spin_in.at[r, :, z])
+                    for r in range(count)
+                    for z in (last, 0)
+                ),
                 (bits_hbm, bits_ref),
                 (beta_hbm, beta_ref),
                 (coup_hbm.at[pl.ds(0, 2)], coup_in.at[pl.ds(0, 2)]),
@@ -146,7 +150,7 @@
         else:
             pl.when(has_below if dt < 0 else has_above)(action)
 
-    for load in loads[:6]:
+    for load in loads[:first]:
         load.start()
 
     barrier = pltpu.get_barrier_semaphore()
@@ -199,11 +203,12 @@
             put_spin(0, r, d, z, 0, jnp.where(e, odd, even))
             put_spin(1, r, d, z, 0, jnp.where(e, even, odd))
 
-    middle = k // chunk // 2 * chunk
+    half, quarter = k // 2, k // 4
 
     def parts(x, r):
-        split = x == HALVES - 1 and r == count - 1 and middle > 0
-        return [(0, middle), (middle, k)] if split else [(0, k)]
+        if x < HALVES - 1 or r < count - 1 or quarter % 8:
+            return [(0, k)]
+        return [(0, half), (half, half + quarter), (half + quarter, k)]
 
     def halo(x, r, side, part=0):
         c = 1 - x % 2
@@ -215,7 +220,7 @@
             src_ref=plain if side == 0 else lifted.at[c, r, :, pl.ds(start, size), :],
             dst_ref=sp.at[c, r, :, above, pl.ds(PAD + start, size), :],
             send_sem=hsend.at[x % 2, r],
-            recv_sem=hrecv.at[2 if part else x % 2, r if part == 0 else 0, side],
+            recv_sem=hrecv.at[part + 1 if part else x % 2, r if part == 0 else 0, side],
             device_id={"gz": down if side == 0 else up},
             device_id_type=MESH,
         )
@@ -242,9 +247,9 @@
             ready()
             pl.semaphore_signal(wrap_sem, inc=1, device_id={"gz": up}, device_id_type=MESH)
 
-    for load in loads[:6]:
+    for load in loads[:4]:
         load.wait()
-    for load in loads[6:]:
+    for load in loads[first : first + 4]:
         load.start()
 
     def pack_edges(r):
@@ -265,6 +270,9 @@
         return jnp.full((1, width), value, jnp.int32).astype(jnp.float32)
 
     for r in range(count):
+        if r > 0:
+            for load in loads[2 * r + 2 : 2 * r + 4]:
+                load.wait()
         pack_edges(r)
         if r == 0:
             if near:
@@ -277,6 +285,11 @@
         else:
             halo(0, r, 0).start()
 
+    for load in loads[first - 2 : first]:
+        load.wait()
+    for load in loads[first + 4 :]:
+        load.start()
+
     tsend[0, 0:1] = wide(slot_order(count - 1))
     tsend[0, 1:2] = wide(bits_ref[count - 1])
     tsend[0, 2:3] = wide(bits_ref[count - 2])
@@ -300,7 +313,7 @@
     along(1, lambda: tell(0).start())
     along(-1, lambda: tell(1).start())
 
-    for load in loads[6:9]:
+    for load in loads[first : first + 3]:
         load.wait()
 
     def pack_bonds(i, carry):
@@ -345,7 +358,7 @@
             for r in range(count):
                 halo(0, r, 0).start()
 
-    def pull(c, r, z, start):
+    def pull(c, r, z, start, chunk=chunk):
         o = 1 - c
         part = pl.ds(start, chunk)
         e = parity(r, z, chunk)
@@ -374,9 +387,10 @@
                     lift(c, r, d, start, value)
 
     def heat(c, r, z, lifting=False, rows_of=(0, k)):
-        for start in range(*rows_of, chunk):
-            part = pl.ds(start, chunk)
-            pulled = pull(c, r, z, start)
+        size = min(chunk, rows_of[1] - rows_of[0])
+        for start in range(*rows_of, size):
+            part = pl.ds(start, size)
+            pulled = pull(c, r, z, start, size)
             trial = [ut[c, r, d, z, part, :] for d in range(3)]
             renewed = heat_bath(pulled, beta_ref[r], lv[c, r, z, part, :], trial)
             for d, value in enumerate(renewed):
@@ -385,7 +399,7 @@
                     lift(c, r, d, start, value)
             if c == 1:
                 terms = dot3(renewed, pulled)
-                eacc[r] = eacc[r] + sum(terms[j : j + 8] for j in range(0, chunk, 8))
+                eacc[r] = eacc[r] + sum(terms[j : j + 8] for j in range(0, size, 8))
 
     def pack_heat(r, z):
         for start in range(0, k, chunk):
@@ -466,23 +480,25 @@
     def work(x):
         return functools.partial(relax if x < relaxing else heat, x % 2)
 
+    ahead = g < n - 1
     eacc[...] = jnp.zeros_like(eacc)
     relaxing = 2 * OR_SWEEPS
     for r in range(count):
         inner(r, work(0))
-    for load in loads[9:]:
+    for load in loads[first + 3 :]:
         load.wait()
     for x in range(HALVES - 1):
         for r in range(count):
             for side, z in ((0, 0), (1, last)):
                 take_halo(x, r, side)
                 work(x)(r, z, lifting=side == 1)
-                if len(parts(x + 1, r)) == 1:
-                    halo(x + 1, r, side).start()
-            if len(parts(x + 1, r)) > 1:
-                for part in (0, 1):
-                    for side in (0, 1):
-                        halo(x + 1, r, side, part).start()
+                if side == 0 and len(parts(x + 1, r)) == 1:
+                    pl.when(ahead)(lambda: halo(x + 1, r, 0).start())
+            for part in range(len(parts(x + 1, r))):
+                if len(parts(x + 1, r)) > 1:
+                    pl.when(ahead)(lambda: halo(x + 1, r, 0, part).start())
+                halo(x + 1, r, 1, part).start()
+                pl.when(~ahead)(lambda: halo(x + 1, r, 0, part).start())
             if r == count - 1 and x == relaxing:
                 for z in (0, last):
                     send_off(0, z)
@@ -495,6 +511,10 @@
 
     x = HALVES - 1
     for r in range(count):
+        if r == count - 1:
+            arrived(True)
+            along(1, lambda: tell(1).wait_recv())
+            along(-1, lambda: tell(0).wait_recv())
         for part, rows_of in enumerate(parts(x, r)):
             for side, z in ((0, 0), (1, last)):
                 halo(x, r, 1 - side, part).wait_recv()
@@ -505,10 +525,6 @@
                     send_off(1, z, part)
     for r in range(count):
         ebuf[1, g, r : r + 1] = jnp.sum(eacc[r], axis=0, keepdims=True)
-
-    arrived(True)
-    along(1, lambda: tell(1).wait_recv())
-    along(-1, lambda: tell(0).wait_recv())
 
     def share(dt, source, there):
         return pltpu.make_async_remote_copy(
@@ -673,9 +689,9 @@
             pltpu.SMEM((count,), f32),
             pltpu.SMEM((count,), jnp.int32),
             pltpu.SMEM((count,), jnp.int32),
-            dma((6,)),
+            dma((2 * count + 4,)),
             dma((2, count)),
-            dma((3, count, 2)),
+            dma((4, count, 2)),
             dma((3,)),
             dma((3,)),
             dma((2,)),

time: 63.6 us -> 63.5 us (level)
  no operation moved by 1% of the time
where the time goes in v4:
time: 63.5 us; the launch traced here: 62.9 us
  Pallas kernels  62.3 us (98%)
  between operations  0.64 us (1%)
    pallas_call x1, Pallas kernels, on_device(): pl.pallas_call(functools.partial(sweep_kernel, dims), out_shape=(pltpu.VM...  61 us

profile of v4, /device:TPU:1, one launch (start us, length us, event | category | flops | bytes accessed | tf_op | source)
XLA Modules:
  0.0 62.9 jit_solution(13858332675038660864)
XLA Ops:
  0.6 61.0 %shard_map.95 = (f32[2,8,3,64,128]{4,3,2,1,0:T(8,128)S(1)}, f32[2,8,3,64,128]{4,3,2,1,0:T(8,128)S(1)}, f32[3,8,128]{2,1,0:T(8,128)S(1)}, f32[3,4,2,128]{3,2,1,0:T(2,128)S(1)}) custom-call(f32[2,3,4,128,128]{4,3,2,1,0:T(8,128)} %spin_hbm.1, f32[3,4,128,128]{3,2,1,0:T(8,128)} %coup_hbm.1, f32[2]{0:T(128)} %beta_hbm.1, s32[2]{0:T(128)} %order_hbm.1, ...), custom_call_target="tpu_custom_call" | custom-call | tf_op jit(solution)/shard_map/pallas_call | solution.py:661
  61.7 1.2 %shard_map.96 = (f32[2,3,4,128,128]{4,3,2,1,0:T(8,128)}, f32[2]{0:T(128)}) custom-call(f32[2,8,3,64,128]{4,3,2,1,0:T(8,128)S(1)} %get-tuple-element.6.evened, f32[2,8,3,64,128]{4,3,2,1,0:T(8,128)S(1)} %get-tuple-element.7.rbuf, f32[3,8,128]{2,1,0:T(8,128)S(1)} %get-tuple-element.8.trecv, f32[3,4,2,128]{3,2,1,0:T(2,128)S(1)} %get-tuple-element.9.ebuf), custom_call_target="tpu_custom_call" | custom-call | tf_op jit(solution)/shard_map/pallas_call | solution.py:707

commit v5 on v4

--- a/solution.py
+++ b/solution.py
@@ -29,6 +29,30 @@
     sine = half * horner(SIN_TERMS, square)
     cosine = horner(COS_TERMS, square)
     return 1.0 - 2.0 * sine * sine, 2.0 * sine * cosine
+
+
+def with_sign(size, like):
+    return jnp.where(like < 0.0, -size, size)
+
+
+def to_square(vector):
+    a, b, c = vector
+    inverse = 1.0 / (jnp.abs(a) + jnp.abs(b) + jnp.abs(c))
+    p, q = a * inverse, b * inverse
+    low = c < 0.0
+    return (
+        jnp.where(low, with_sign(1.0 - jnp.abs(q), p), p),
+        jnp.where(low, with_sign(1.0 - jnp.abs(p), q), q),
+    )
+
+
+def from_square(p, q):
+    c = 1.0 - jnp.abs(p) - jnp.abs(q)
+    low = c < 0.0
+    a = jnp.where(low, with_sign(1.0 - jnp.abs(q), p), p)
+    b = jnp.where(low, with_sign(1.0 - jnp.abs(p), q), q)
+    inverse = 1.0 / jnp.sqrt(a * a + b * b + c * c)
+    return a * inverse, b * inverse, c * inverse
 
 
 def dot3(a, b):
@@ -79,6 +103,9 @@
     height_in,
     angle_in,
     lifted,
+    osend,
+    orecv,
+    cbelow,
     sp,
     xo,
     xr,
@@ -102,6 +129,7 @@
     trsem,
     xsend,
     xrecv,
+    csem,
     wrap_sem,
 ):
     count, planes, rows, width, n, m = dims
@@ -155,29 +183,20 @@
 
     barrier = pltpu.get_barrier_semaphore()
 
-    def greet(dt, there):
-        pl.semaphore_signal(barrier, inc=1, device_id=peer(dt, there), device_id_type=MESH)
-
-    sides = has_below.astype(jnp.int32) + has_above.astype(jnp.int32)
+    def greet(temp, there):
+        target = {"temp": temp, "gz": there}
+        pl.semaphore_signal(barrier, inc=1, device_id=target, device_id_type=MESH)
+
     if near:
-
-        @pl.when(g < n - 1)
-        def _():
-            greet(0, up)
-
-        greet(0, down)
-        along(-1, lambda: greet(-1, g))
-        along(1, lambda: greet(1, g))
-        expected = sides + jnp.where(g == 0, 1, 2)
+        pl.when(g < n - 1)(lambda: greet(t, up))
+        greet(t, down)
+        for d in range(1, m):
+            greet(lax.rem(t + d, m), g)
+        expected = m - 1 + jnp.where(g == 0, 1, 2)
     else:
-        for dt in (-1, 0, 1):
-
-            def greet_all(dt=dt):
-                for d in range(1 if dt == 0 else 0, n):
-                    greet(dt, lax.rem(g + d, n))
-
-            along(dt, greet_all)
-        expected = n - 1 + n * sides
+        for i in range(1, n * m):
+            greet(lax.rem(t + i // n, m), lax.rem(g + i % n, n))
+        expected = n * m - 1
 
     def parity(r, z, size):
         lane = lax.broadcasted_iota(jnp.int32, (size, width), 1)
@@ -225,8 +244,47 @@
             device_id_type=MESH,
         )
 
+    def opening(r, side):
+        return pltpu.make_async_remote_copy(
+            src_ref=osend.at[r, side],
+            dst_ref=orecv.at[r, side],
+            send_sem=hsend.at[0, r],
+            recv_sem=hrecv.at[0, r, side],
+            device_id={"gz": down if side == 0 else up},
+            device_id_type=MESH,
+        )
+
+    shares_of = m if rows % (8 * m) == 0 else 1
+    size_of = rows // shares_of
+    stretch = pl.ds(pl.multiple_of(t * size_of, 8) if shares_of > 1 else 0, size_of)
+
+    def across():
+        return pltpu.make_async_remote_copy(
+            src_ref=coup_in.at[2, last, stretch],
+            dst_ref=cbelow.at[stretch],
+            send_sem=csem.at[0],
+            recv_sem=csem.at[1],
+            device_id={"gz": up},
+            device_id_type=MESH,
+        )
+
+    def pass_on(d):
+        return pltpu.make_async_remote_copy(
+            src_ref=cbelow.at[stretch],
+            dst_ref=cbelow.at[stretch],
+            send_sem=csem.at[2],
+            recv_sem=csem.at[3],
+            device_id={"temp": lax.rem(t + d, m)},
+            device_id_type=MESH,
+        )
+
+    def passed_on(i):
+        if shares_of > 1:
+            ref = cbelow.at[pl.ds(0, (m - 1) * size_of)]
+            pltpu.make_async_copy(ref, ref, csem.at[i]).wait()
+
     def sent(x, r):
-        both = lifted.at[:, r]
+        both = lifted.at[:, r] if x else osend.at[r]
         pltpu.make_async_copy(both, both, hsend.at[x % 2, r]).wait()
 
     def lift(c, r, d, start, value):
@@ -249,6 +307,8 @@
 
     for load in loads[:4]:
         load.wait()
+    if near:
+        pl.when(g == n - 1)(lambda: across().start())
     for load in loads[first : first + 4]:
         load.start()
 
@@ -257,10 +317,10 @@
         even, odd = halves(coup_in, (2, last), 0, k)
         zu[0, r, last] = jnp.where(e, odd, even)
         zu[1, r, last] = jnp.where(e, even, odd)
-        pack_spin(r, last)
-        for d in range(3):
-            lift(1, r, d, 0, sp[1, r, d, planes, pl.ds(PAD, k), :])
-        pack_spin(r, 0)
+        for side, z in ((1, last), (0, 0)):
+            pack_spin(r, z)
+            edge = to_square([sp[1, r, d, z + 1, pl.ds(PAD, k), :] for d in range(3)])
+            osend[r, side, 0], osend[r, side, 1] = edge
 
     def slot_order(r):
         other = order_ref[r ^ 1]
@@ -276,14 +336,20 @@
         pack_edges(r)
         if r == 0:
             if near:
-                pl.when(g < n - 1)(ready)
+
+                @pl.when(g < n - 1)
+                def _():
+                    ready()
+                    across().start()
+
             else:
                 ready()
-        halo(0, r, 1).start()
+                across().start()
+        opening(r, 1).start()
         if near:
-            pl.when(g > 0)(lambda: halo(0, r, 0).start())
+            pl.when(g > 0)(lambda: opening(r, 0).start())
         else:
-            halo(0, r, 0).start()
+            opening(r, 0).start()
 
     for load in loads[first - 2 : first]:
         load.wait()
@@ -356,7 +422,7 @@
         def _():
             pl.semaphore_wait(wrap_sem, 1)
             for r in range(count):
-                halo(0, r, 0).start()
+                opening(r, 0).start()
 
     def pull(c, r, z, start, chunk=chunk):
         o = 1 - c
@@ -421,8 +487,18 @@
 
     def take_halo(x, r, side):
         halo(x, r, 1 - side).wait_recv()
-        if x >= 1 and side == 0:
+        if side == 0:
             sent(x - 1, r)
+
+    def take_opening(r, side):
+        opening(r, 1 - side).wait_recv()
+        vector = from_square(orecv[r, 1 - side, 0], orecv[r, 1 - side, 1])
+        if side == 0:
+            even, odd = halves(cbelow, (), 0, k)
+            bond = jnp.where(parity(r, 0, k), odd, even)
+            vector = [bond * v for v in vector]
+        for d in range(3):
+            sp[1, r, d, planes + 1 if side else 0, pl.ds(PAD, k), :] = vector[d]
 
     def settle(c, z, start, stop):
         size = stop - start
@@ -487,14 +563,25 @@
         inner(r, work(0))
     for load in loads[first + 3 :]:
         load.wait()
+    across().wait_recv()
+    if shares_of > 1:
+        for d in range(1, m):
+            pass_on(d).start()
     for x in range(HALVES - 1):
         for r in range(count):
-            for side, z in ((0, 0), (1, last)):
-                take_halo(x, r, side)
+            for side, z in ((0, 0), (1, last)) if x else ((1, last), (0, 0)):
+                if x:
+                    take_halo(x, r, side)
+                else:
+                    if r == 0 and side == 0:
+                        passed_on(3)
+                    take_opening(r, side)
                 work(x)(r, z, lifting=side == 1)
-                if side == 0 and len(parts(x + 1, r)) == 1:
+                if x == 0:
+                    halo(1, r, side).start()
+                elif side == 0 and len(parts(x + 1, r)) == 1:
                     pl.when(ahead)(lambda: halo(x + 1, r, 0).start())
-            for part in range(len(parts(x + 1, r))):
+            for part in range(len(parts(x + 1, r)) if x else 0):
                 if len(parts(x + 1, r)) > 1:
                     pl.when(ahead)(lambda: halo(x + 1, r, 0, part).start())
                 halo(x + 1, r, 1, part).start()
@@ -548,6 +635,8 @@
         along(dt, lambda dt=dt: spread(dt))
     for r in range(count):
         sent(x, r)
+    across().wait_send()
+    passed_on(2)
     along(1, lambda: tell(0).wait_send())
     along(-1, lambda: tell(1).wait_send())
     both_ways(lambda side: whole(side, 2 * planes, xsend.at[side]))
@@ -675,6 +764,9 @@
             pltpu.VMEM(level.shape, f32),
             pltpu.VMEM(level.shape, f32),
             pltpu.VMEM((2, count, 3, k, width), f32),
+            pltpu.VMEM((count, 2, 2, k, width), f32),
+            pltpu.VMEM((count, 2, 2, k, width), f32),
+            pltpu.VMEM((rows, width), f32),
             pltpu.VMEM((2, count, 3, planes + 2, k + 2 * PAD, width), f32),
             bonds,
             bonds,
@@ -698,6 +790,7 @@
             dma((2,)),
             dma((2,)),
             dma((2, 2)),
+            dma((4,)),
             pltpu.SemaphoreType.REGULAR,
         ],
         compiler_params=pltpu.CompilerParams(

time: 63.5 us -> 60.7 us (0.956)
  Pallas kernels: 62.3 us -> 59.8 us
    pallas_call x1, Pallas kernels: 61 us -> 58.6 us  [on_device(): pl.pallas_call(functools.partial(sweep_kernel, dims), out_shape=(pltpu.VM...]
where the time goes in v5:
time: 60.7 us; the launch traced here: 60.5 us
  Pallas kernels  59.8 us (99%)
  between operations  0.64 us (1%)
    pallas_call x1, Pallas kernels, on_device(): pl.pallas_call(functools.partial(sweep_kernel, dims), out_shape=(pltpu.VM...  58.6 us
    pallas_call x1, Pallas kernels, on_device(): pl.pallas_call(functools.partial(finish_kernel, dims), out_shape=(jax.Sha...  1.25 us

profile of v5, /device:TPU:1, one launch (start us, length us, event | category | flops | bytes accessed | tf_op | source)
XLA Modules:
  0.0 60.5 jit_solution(73634466473384179)
XLA Ops:
  0.6 58.6 %shard_map.95 = (f32[2,8,3,64,128]{4,3,2,1,0:T(8,128)S(1)}, f32[2,8,3,64,128]{4,3,2,1,0:T(8,128)S(1)}, f32[3,8,128]{2,1,0:T(8,128)S(1)}, f32[3,4,2,128]{3,2,1,0:T(2,128)S(1)}) custom-call(f32[2,3,4,128,128]{4,3,2,1,0:T(8,128)} %spin_hbm.1, f32[3,4,128,128]{3,2,1,0:T(8,128)} %coup_hbm.1, f32[2]{0:T(128)} %beta_hbm.1, s32[2]{0:T(128)} %order_hbm.1, ...), custom_call_target="tpu_custom_call" | custom-call | tf_op jit(solution)/shard_map/pallas_call | solution.py:750
  59.2 1.2 %shard_map.96 = (f32[2,3,4,128,128]{4,3,2,1,0:T(8,128)}, f32[2]{0:T(128)}) custom-call(f32[2,8,3,64,128]{4,3,2,1,0:T(8,128)S(1)} %get-tuple-element.6.evened, f32[2,8,3,64,128]{4,3,2,1,0:T(8,128)S(1)} %get-tuple-element.7.rbuf, f32[3,8,128]{2,1,0:T(8,128)S(1)} %get-tuple-element.8.trecv, f32[3,4,2,128]{3,2,1,0:T(2,128)S(1)} %get-tuple-element.9.ebuf), custom_call_target="tpu_custom_call" | custom-call | tf_op jit(solution)/shard_map/pallas_call | solution.py:800

commit v6 on v5

--- a/solution.py
+++ b/solution.py
@@ -225,7 +225,7 @@
     half, quarter = k // 2, k // 4
 
     def parts(x, r):
-        if x < HALVES - 1 or r < count - 1 or quarter % 8:
+        if x < HALVES - 1 or quarter % 8 or r < count - 1:
             return [(0, k)]
         return [(0, half), (half, half + quarter), (half + quarter, k)]
 
@@ -295,20 +295,8 @@
         if planes > 2:
             lax.fori_loop(1, last, lambda z, carry: (action(r, z), carry)[1], 0)
 
-    def ready():
-        pl.semaphore_wait(barrier, expected)
-
-    if near:
-
-        @pl.when(g == n - 1)
-        def _():
-            ready()
-            pl.semaphore_signal(wrap_sem, inc=1, device_id={"gz": up}, device_id_type=MESH)
-
     for load in loads[:4]:
         load.wait()
-    if near:
-        pl.when(g == n - 1)(lambda: across().start())
     for load in loads[first : first + 4]:
         load.start()
 
@@ -335,16 +323,14 @@
                 load.wait()
         pack_edges(r)
         if r == 0:
+            pl.semaphore_wait(barrier, expected)
             if near:
 
-                @pl.when(g < n - 1)
+                @pl.when(g == n - 1)
                 def _():
-                    ready()
-                    across().start()
-
-            else:
-                ready()
-                across().start()
+                    pl.semaphore_signal(wrap_sem, inc=1, device_id={"gz": up}, device_id_type=MESH)
+
+            across().start()
         opening(r, 1).start()
         if near:
             pl.when(g > 0)(lambda: opening(r, 0).start())
@@ -567,19 +553,37 @@
     if shares_of > 1:
         for d in range(1, m):
             pass_on(d).start()
+
+    ends = (g == 0) | (g == n - 1)
+    outer = jnp.where(g == n - 1, 0, 1)
+    bonds_at = jnp.where(g == 0, count, jnp.where(g == n - 1, 0, 1))
+
+    def first_step(i, carry):
+        r = jnp.where(ends, lax.rem(i, count), i // 2)
+        side = jnp.where(ends, jnp.where(i < count, outer, 1 - outer), 1 - lax.rem(i, 2))
+        pl.when(i == bonds_at)(lambda: passed_on(3))
+
+        @pl.when(side == 1)
+        def _():
+            take_opening(r, 1)
+            work(0)(r, last, lifting=True)
+            halo(1, r, 1).start()
+
+        @pl.when(side == 0)
+        def _():
+            take_opening(r, 0)
+            work(0)(r, 0)
+            halo(1, r, 0).start()
+
+        return carry
+
+    lax.fori_loop(0, 2 * count, first_step, 0)
     for x in range(HALVES - 1):
         for r in range(count):
-            for side, z in ((0, 0), (1, last)) if x else ((1, last), (0, 0)):
-                if x:
-                    take_halo(x, r, side)
-                else:
-                    if r == 0 and side == 0:
-                        passed_on(3)
-                    take_opening(r, side)
+            for side, z in ((0, 0), (1, last)) if x else ():
+                take_halo(x, r, side)
                 work(x)(r, z, lifting=side == 1)
-                if x == 0:
-                    halo(1, r, side).start()
-                elif side == 0 and len(parts(x + 1, r)) == 1:
+                if side == 0 and len(parts(x + 1, r)) == 1:
                     pl.when(ahead)(lambda: halo(x + 1, r, 0).start())
             for part in range(len(parts(x + 1, r)) if x else 0):
                 if len(parts(x + 1, r)) > 1:

time: 60.7 us -> 62.2 us (1.025)
  Pallas kernels: 59.8 us -> 61.2 us
    pallas_call x1, Pallas kernels: 58.6 us -> 59.9 us  [on_device(): pl.pallas_call(functools.partial(sweep_kernel, dims), out_shape=(pltpu.VM...]
where the time goes in v6:
time: 62.2 us; the launch traced here: 61.8 us
  Pallas kernels  61.2 us (98%)
  between operations  0.64 us (1%)
    pallas_call x1, Pallas kernels, on_device(): pl.pallas_call(functools.partial(sweep_kernel, dims), out_shape=(pltpu.VM...  59.9 us
    pallas_call x1, Pallas kernels, on_device(): pl.pallas_call(functools.partial(finish_kernel, dims), out_shape=(jax.Sha...  1.25 us

profile of v6, /device:TPU:1, one launch (start us, length us, event | category | flops | bytes accessed | tf_op | source)
XLA Modules:
  0.0 61.8 jit_solution(14879127156370444140)
XLA Ops:
  0.6 59.9 %shard_map.95 = (f32[2,8,3,64,128]{4,3,2,1,0:T(8,128)S(1)}, f32[2,8,3,64,128]{4,3,2,1,0:T(8,128)S(1)}, f32[3,8,128]{2,1,0:T(8,128)S(1)}, f32[3,4,2,128]{3,2,1,0:T(2,128)S(1)}) custom-call(f32[2,3,4,128,128]{4,3,2,1,0:T(8,128)} %spin_hbm.1, f32[3,4,128,128]{3,2,1,0:T(8,128)} %coup_hbm.1, f32[2]{0:T(128)} %beta_hbm.1, s32[2]{0:T(128)} %order_hbm.1, ...), custom_call_target="tpu_custom_call" | custom-call | tf_op jit(solution)/shard_map/pallas_call | solution.py:754
  60.6 1.2 %shard_map.96 = (f32[2,3,4,128,128]{4,3,2,1,0:T(8,128)}, f32[2]{0:T(128)}) custom-call(f32[2,8,3,64,128]{4,3,2,1,0:T(8,128)S(1)} %get-tuple-element.6.evened, f32[2,8,3,64,128]{4,3,2,1,0:T(8,128)S(1)} %get-tuple-element.7.rbuf, f32[3,8,128]{2,1,0:T(8,128)S(1)} %get-tuple-element.8.trecv, f32[3,4,2,128]{3,2,1,0:T(2,128)S(1)} %get-tuple-element.9.ebuf), custom_call_target="tpu_custom_call" | custom-call | tf_op jit(solution)/shard_map/pallas_call | solution.py:804

commit v7 on v5

--- a/solution.py
+++ b/solution.py
@@ -131,6 +131,7 @@
     xrecv,
     csem,
     wrap_sem,
+    temp_sem,
 ):
     count, planes, rows, width, n, m = dims
     k = rows // 2
@@ -191,8 +192,8 @@
         pl.when(g < n - 1)(lambda: greet(t, up))
         greet(t, down)
         for d in range(1, m):
-            greet(lax.rem(t + d, m), g)
-        expected = m - 1 + jnp.where(g == 0, 1, 2)
+            pl.when(t + d < m)(lambda: greet(t + d, g))
+        expected = t + jnp.where(g == 0, 1, 2)
     else:
         for i in range(1, n * m):
             greet(lax.rem(t + i // n, m), lax.rem(g + i % n, n))
@@ -376,8 +377,14 @@
             device_id_type=MESH,
         )
 
-    along(1, lambda: tell(0).start())
-    along(-1, lambda: tell(1).start())
+    if near:
+        for d in range(1, m):
+
+            @pl.when(t >= d)
+            def _():
+                target = {"temp": t - d, "gz": g}
+                pl.semaphore_signal(temp_sem, inc=1, device_id=target, device_id_type=MESH)
+
 
     for load in loads[first : first + 3]:
         load.wait()
@@ -563,6 +570,10 @@
         inner(r, work(0))
     for load in loads[first + 3 :]:
         load.wait()
+    if near:
+        along(1, lambda: pl.semaphore_wait(temp_sem, m - 1 - t))
+    along(1, lambda: tell(0).start())
+    along(-1, lambda: tell(1).start())
     across().wait_recv()
     if shares_of > 1:
         for d in range(1, m):
@@ -792,6 +803,7 @@
             dma((2, 2)),
             dma((4,)),
             pltpu.SemaphoreType.REGULAR,
+            pltpu.SemaphoreType.REGULAR,
         ],
         compiler_params=pltpu.CompilerParams(
             collective_id=0, has_side_effects=True, vmem_limit_bytes=58 * 1024 * 1024

time: 60.7 us -> 60.7 us (level)
  no operation moved by 1% of the time
where the time goes in v7:
time: 60.7 us; the launch traced here: 60.3 us
  Pallas kernels  59.6 us (98%)
  between operations  0.64 us (1%)
    pallas_call x1, Pallas kernels, on_device(): pl.pallas_call(functools.partial(sweep_kernel, dims), out_shape=(pltpu.VM...  58.4 us
    pallas_call x1, Pallas kernels, on_device(): pl.pallas_call(functools.partial(finish_kernel, dims), out_shape=(jax.Sha...  1.25 us

profile of v7, /device:TPU:1, one launch (start us, length us, event | category | flops | bytes accessed | tf_op | source)
XLA Modules:
  0.0 60.3 jit_solution(6946869581997964731)
XLA Ops:
  0.6 58.4 %shard_map.95 = (f32[2,8,3,64,128]{4,3,2,1,0:T(8,128)S(1)}, f32[2,8,3,64,128]{4,3,2,1,0:T(8,128)S(1)}, f32[3,8,128]{2,1,0:T(8,128)S(1)}, f32[3,4,2,128]{3,2,1,0:T(2,128)S(1)}) custom-call(f32[2,3,4,128,128]{4,3,2,1,0:T(8,128)} %spin_hbm.1, f32[3,4,128,128]{3,2,1,0:T(8,128)} %coup_hbm.1, f32[2]{0:T(128)} %beta_hbm.1, s32[2]{0:T(128)} %order_hbm.1, ...), custom_call_target="tpu_custom_call" | custom-call | tf_op jit(solution)/shard_map/pallas_call | solution.py:761
  59.0 1.2 %shard_map.96 = (f32[2,3,4,128,128]{4,3,2,1,0:T(8,128)}, f32[2]{0:T(128)}) custom-call(f32[2,8,3,64,128]{4,3,2,1,0:T(8,128)S(1)} %get-tuple-element.6.evened, f32[2,8,3,64,128]{4,3,2,1,0:T(8,128)S(1)} %get-tuple-element.7.rbuf, f32[3,8,128]{2,1,0:T(8,128)S(1)} %get-tuple-element.8.trecv, f32[3,4,2,128]{3,2,1,0:T(2,128)S(1)} %get-tuple-element.9.ebuf), custom_call_target="tpu_custom_call" | custom-call | tf_op jit(solution)/shard_map/pallas_call | solution.py:812

commit v8 on v7

--- a/solution.py
+++ b/solution.py
@@ -226,7 +226,7 @@
     half, quarter = k // 2, k // 4
 
     def parts(x, r):
-        if x < HALVES - 1 or r < count - 1 or quarter % 8:
+        if x < HALVES - 1 or quarter % 8 or r < count - 1:
             return [(0, k)]
         return [(0, half), (half, half + quarter), (half + quarter, k)]
 
@@ -578,19 +578,33 @@
     if shares_of > 1:
         for d in range(1, m):
             pass_on(d).start()
+
+    def first_step(i, carry):
+        r = jnp.where(g == 0, lax.rem(i, count), i // 2)
+        side = jnp.where(g == 0, jnp.where(i < count, 1, 0), 1 - lax.rem(i, 2))
+        pl.when(i == jnp.where(g == 0, count, 1))(lambda: passed_on(3))
+
+        @pl.when(side == 1)
+        def _():
+            take_opening(r, 1)
+            work(0)(r, last, lifting=True)
+            halo(1, r, 1).start()
+
+        @pl.when(side == 0)
+        def _():
+            take_opening(r, 0)
+            work(0)(r, 0)
+            halo(1, r, 0).start()
+
+        return carry
+
+    lax.fori_loop(0, 2 * count, first_step, 0)
     for x in range(HALVES - 1):
         for r in range(count):
-            for side, z in ((0, 0), (1, last)) if x else ((1, last), (0, 0)):
-                if x:
-                    take_halo(x, r, side)
-                else:
-                    if r == 0 and side == 0:
-                        passed_on(3)
-                    take_opening(r, side)
+            for side, z in ((0, 0), (1, last)) if x else ():
+                take_halo(x, r, side)
                 work(x)(r, z, lifting=side == 1)
-                if x == 0:
-                    halo(1, r, side).start()
-                elif side == 0 and len(parts(x + 1, r)) == 1:
+                if side == 0 and len(parts(x + 1, r)) == 1:
                     pl.when(ahead)(lambda: halo(x + 1, r, 0).start())
             for part in range(len(parts(x + 1, r)) if x else 0):
                 if len(parts(x + 1, r)) > 1:
@@ -704,6 +718,24 @@
         jnp.where(take > 0.5, order, own_order(r)).astype(jnp.int32)
         for r, (_, take, order) in enumerate(plans)
     ]
+    def unpack(z):
+        for r in range(count):
+            other, take, _ = plans[r]
+            taking = mask(take, k)
+            e = ((lane + (jnp.broadcast_to(orders[r], (k, width)) + (g * planes + z))) & 1) != 0
+            for d in range(3):
+                first, second = [
+                    jnp.where(taking, other[i, d], evened[r, i, d]) for i in (z, planes + z)
+                ]
+                stage[r, d, z, pl.ds(0, k, stride=2), :] = jnp.where(e, second, first)
+                stage[r, d, z, pl.ds(1, k, stride=2), :] = jnp.where(e, first, second)
+            copy = pltpu.make_async_copy(
+                stage.at[r, :, z], out_hbm.at[r, :, z], out_sem
+            )
+            copy.start()
+
+    for z in range(planes // 2):
+        unpack(z)
     sites = float(width * rows * planes * n)
 
     def total(slot, r):
@@ -730,21 +762,8 @@
         eout_ref[r] = jnp.max(jnp.where(take > 0.5, partner, energy[r]))
     told = pltpu.make_async_copy(eout_ref, eout_hbm, eout_sem)
     told.start()
-    for z in range(planes):
-        for r in range(count):
-            other, take, _ = plans[r]
-            taking = mask(take, k)
-            e = ((lane + (jnp.broadcast_to(orders[r], (k, width)) + (g * planes + z))) & 1) != 0
-            for d in range(3):
-                first, second = [
-                    jnp.where(taking, other[i, d], evened[r, i, d]) for i in (z, planes + z)
-                ]
-                stage[r, d, z, pl.ds(0, k, stride=2), :] = jnp.where(e, second, first)
-                stage[r, d, z, pl.ds(1, k, stride=2), :] = jnp.where(e, first, second)
-            copy = pltpu.make_async_copy(
-                stage.at[r, :, z], out_hbm.at[r, :, z], out_sem
-            )
-            copy.start()
+    for z in range(planes // 2, planes):
+        unpack(z)
     told.wait()
     pltpu.make_async_copy(stage, out_hbm, out_sem).wait()
 

time: 60.7 us -> 60.6 us (level)
  no operation moved by 1% of the time
where the time goes in v8:
time: 60.6 us; the launch traced here: 60.4 us
  Pallas kernels  59.8 us (99%)
  between operations  0.64 us (1%)
    pallas_call x1, Pallas kernels, on_device(): pl.pallas_call(functools.partial(sweep_kernel, dims), out_shape=(pltpu.VM...  58.5 us
    pallas_call x1, Pallas kernels, on_device(): pl.pallas_call(functools.partial(finish_kernel, dims), out_shape=(jax.Sha...  1.25 us

profile of v8, /device:TPU:1, one launch (start us, length us, event | category | flops | bytes accessed | tf_op | source)
XLA Modules:
  0.0 60.4 jit_solution(11046589098387484944)
XLA Ops:
  0.6 58.5 %shard_map.95 = (f32[2,8,3,64,128]{4,3,2,1,0:T(8,128)S(1)}, f32[2,8,3,64,128]{4,3,2,1,0:T(8,128)S(1)}, f32[3,8,128]{2,1,0:T(8,128)S(1)}, f32[3,4,2,128]{3,2,1,0:T(2,128)S(1)}) custom-call(f32[2,3,4,128,128]{4,3,2,1,0:T(8,128)} %spin_hbm.1, f32[3,4,128,128]{3,2,1,0:T(8,128)} %coup_hbm.1, f32[2]{0:T(128)} %beta_hbm.1, s32[2]{0:T(128)} %order_hbm.1, ...), custom_call_target="tpu_custom_call" | custom-call | tf_op jit(solution)/shard_map/pallas_call | solution.py:780
  59.2 1.2 %shard_map.96 = (f32[2,3,4,128,128]{4,3,2,1,0:T(8,128)}, f32[2]{0:T(128)}) custom-call(f32[2,8,3,64,128]{4,3,2,1,0:T(8,128)S(1)} %get-tuple-element.6.evened, f32[2,8,3,64,128]{4,3,2,1,0:T(8,128)S(1)} %get-tuple-element.7.rbuf, f32[3,8,128]{2,1,0:T(8,128)S(1)} %get-tuple-element.8.trecv, f32[3,4,2,128]{3,2,1,0:T(2,128)S(1)} %get-tuple-element.9.ebuf), custom_call_target="tpu_custom_call" | custom-call | tf_op jit(solution)/shard_map/pallas_call | solution.py:831

commit v9 on v8

--- a/solution.py
+++ b/solution.py
@@ -179,7 +179,7 @@
         else:
             pl.when(has_below if dt < 0 else has_above)(action)
 
-    for load in loads[:first]:
+    for load in loads[:4]:
         load.start()
 
     barrier = pltpu.get_barrier_semaphore()
@@ -223,12 +223,12 @@
             put_spin(0, r, d, z, 0, jnp.where(e, odd, even))
             put_spin(1, r, d, z, 0, jnp.where(e, even, odd))
 
-    half, quarter = k // 2, k // 4
+    half = k // 2
 
     def parts(x, r):
-        if x < HALVES - 1 or quarter % 8 or r < count - 1:
+        if x < HALVES - 1 or k % 32 or r < count - 1:
             return [(0, k)]
-        return [(0, half), (half, half + quarter), (half + quarter, k)]
+        return [(0, half), (half, k - 8), (k - 8, k)]
 
     def halo(x, r, side, part=0):
         c = 1 - x % 2
@@ -240,7 +240,9 @@
             src_ref=plain if side == 0 else lifted.at[c, r, :, pl.ds(start, size), :],
             dst_ref=sp.at[c, r, :, above, pl.ds(PAD + start, size), :],
             send_sem=hsend.at[x % 2, r],
-            recv_sem=hrecv.at[part + 1 if part else x % 2, r if part == 0 else 0, side],
+            recv_sem=hrecv.at[
+                4 * count + 2 * part - 2 + side if part else 2 * (x % 2 * count + r) + side
+            ],
             device_id={"gz": down if side == 0 else up},
             device_id_type=MESH,
         )
@@ -250,7 +252,7 @@
             src_ref=osend.at[r, side],
             dst_ref=orecv.at[r, side],
             send_sem=hsend.at[0, r],
-            recv_sem=hrecv.at[0, r, side],
+            recv_sem=hrecv.at[2 * r + side],
             device_id={"gz": down if side == 0 else up},
             device_id_type=MESH,
         )
@@ -310,7 +312,7 @@
         load.wait()
     if near:
         pl.when(g == n - 1)(lambda: across().start())
-    for load in loads[first : first + 4]:
+    for load in loads[4 : first + 4]:
         load.start()
 
     def pack_edges(r):
@@ -628,9 +630,9 @@
             along(1, lambda: tell(1).wait_recv())
             along(-1, lambda: tell(0).wait_recv())
         for part, rows_of in enumerate(parts(x, r)):
-            for side, z in ((0, 0), (1, last)):
+            for side, z in ((1, last), (0, 0)):
                 halo(x, r, 1 - side, part).wait_recv()
-                if part == 0 and side == 0:
+                if part == 0 and side == 1:
                     sent(x - 1, r)
                 work(x)(r, z, rows_of=rows_of)
                 if r == count - 1:
@@ -813,7 +815,7 @@
             pltpu.SMEM((count,), jnp.int32),
             dma((2 * count + 4,)),
             dma((2, count)),
-            dma((4, count, 2)),
+            dma((4 * count + 4,)),
             dma((3,)),
             dma((3,)),
             dma((2,)),

time: 60.6 us -> 60.4 us (level)
  no operation moved by 1% of the time
where the time goes in v9:
time: 60.4 us; the launch traced here: 60.3 us
  Pallas kernels  59.6 us (99%)
  between operations  0.64 us (1%)
    pallas_call x1, Pallas kernels, on_device(): pl.pallas_call(functools.partial(sweep_kernel, dims), out_shape=(pltpu.VM...  58.4 us
    pallas_call x1, Pallas kernels, on_device(): pl.pallas_call(functools.partial(finish_kernel, dims), out_shape=(jax.Sha...  1.25 us

profile of v9, /device:TPU:1, one launch (start us, length us, event | category | flops | bytes accessed | tf_op | source)
XLA Modules:
  0.0 60.3 jit_solution(2111729362030265613)
XLA Ops:
  0.6 58.4 %shard_map.95 = (f32[2,8,3,64,128]{4,3,2,1,0:T(8,128)S(1)}, f32[2,8,3,64,128]{4,3,2,1,0:T(8,128)S(1)}, f32[3,8,128]{2,1,0:T(8,128)S(1)}, f32[3,4,2,128]{3,2,1,0:T(2,128)S(1)}) custom-call(f32[2,3,4,128,128]{4,3,2,1,0:T(8,128)} %spin_hbm.1, f32[3,4,128,128]{3,2,1,0:T(8,128)} %coup_hbm.1, f32[2]{0:T(128)} %beta_hbm.1, s32[2]{0:T(128)} %order_hbm.1, ...), custom_call_target="tpu_custom_call" | custom-call | tf_op jit(solution)/shard_map/pallas_call | solution.py:782
  59.0 1.2 %shard_map.96 = (f32[2,3,4,128,128]{4,3,2,1,0:T(8,128)}, f32[2]{0:T(128)}) custom-call(f32[2,8,3,64,128]{4,3,2,1,0:T(8,128)S(1)} %get-tuple-element.6.evened, f32[2,8,3,64,128]{4,3,2,1,0:T(8,128)S(1)} %get-tuple-element.7.rbuf, f32[3,8,128]{2,1,0:T(8,128)S(1)} %get-tuple-element.8.trecv, f32[3,4,2,128]{3,2,1,0:T(2,128)S(1)} %get-tuple-element.9.ebuf), custom_call_target="tpu_custom_call" | custom-call | tf_op jit(solution)/shard_map/pallas_call | solution.py:833

commit v10 on v9

--- a/solution.py
+++ b/solution.py
@@ -638,14 +638,14 @@
                 if r == count - 1:
                     send_off(1, z, part)
     for r in range(count):
-        ebuf[1, g, r : r + 1] = jnp.sum(eacc[r], axis=0, keepdims=True)
+        ebuf[n + g, r : r + 1] = jnp.sum(eacc[r], axis=0, keepdims=True)
 
     def share(dt, source, there):
         return pltpu.make_async_remote_copy(
-            src_ref=ebuf.at[1, source],
-            dst_ref=ebuf.at[1 - dt, source],
-            send_sem=esend.at[1 - dt],
-            recv_sem=erecv.at[1 - dt],
+            src_ref=ebuf.at[n + source],
+            dst_ref=ebuf.at[(1 - dt) * n + source],
+            send_sem=esend,
+            recv_sem=erecv,
             device_id=peer(dt, there),
             device_id_type=MESH,
         )
@@ -654,9 +654,17 @@
         for d in range(1 if dt == 0 else 0, n):
             share(dt, g, lax.rem(g + d, n)).start()
 
-    def shares(dt, sem):
-        ref = ebuf.at[1, pl.ds(0, n - 1 if dt == 0 else n)]
-        pltpu.make_async_copy(ref, ref, sem).wait()
+    temps = 1 + has_below.astype(jnp.int32) + has_above.astype(jnp.int32)
+
+    def shares(sem):
+        for groups in range(1, 4):
+            size = groups * n - 1
+
+            @pl.when(temps == groups)
+            def _():
+                if size:
+                    ref = ebuf.at[pl.ds(0, size)]
+                    pltpu.make_async_copy(ref, ref, sem).wait()
 
     for dt in (0, 1, -1):
         along(dt, lambda dt=dt: spread(dt))
@@ -668,9 +676,8 @@
     along(-1, lambda: tell(1).wait_send())
     both_ways(lambda side: whole(side, 2 * planes, xsend.at[side]))
     arrived(False)
-    for dt in (0, 1, -1):
-        along(dt, lambda dt=dt: shares(dt, esend.at[1 - dt]))
-        along(dt, lambda dt=dt: shares(dt, erecv.at[1 + dt]))
+    shares(esend)
+    shares(erecv)
 
 
 def finish_kernel(
@@ -741,9 +748,9 @@
     sites = float(width * rows * planes * n)
 
     def total(slot, r):
-        summed = ebuf[slot, 0, r : r + 1]
+        summed = ebuf[slot * n, r : r + 1]
         for j in range(1, n):
-            summed = summed + ebuf[slot, j, r : r + 1]
+            summed = summed + ebuf[slot * n + j, r : r + 1]
         return jnp.broadcast_to(jnp.sum(-summed, axis=1, keepdims=True) / sites, (1, width))
 
     energy = []
@@ -785,7 +792,7 @@
             pltpu.VMEM((count, 2 * planes, 3, k, width), f32),
             pltpu.VMEM((2, 2 * planes, 3, k, width), f32),
             pltpu.VMEM((3, max(8, 2 * count), width), f32),
-            pltpu.VMEM((3, n, count, width), f32),
+            pltpu.VMEM((3 * n, count, width), f32),
         ),
         in_specs=[hbm] * 8,
         out_specs=(vmem,) * 4,
@@ -816,8 +823,8 @@
             dma((2 * count + 4,)),
             dma((2, count)),
             dma((4 * count + 4,)),
-            dma((3,)),
-            dma((3,)),
+            dma(()),
+            dma(()),
             dma((2,)),
             dma((2,)),
             dma((2,)),

time: 60.4 us -> 60.4 us (level)
  no operation moved by 1% of the time
where the time goes in v10:
time: 60.4 us; the launch traced here: 60.2 us
  Pallas kernels  59.6 us (99%)
  between operations  0.64 us (1%)
    pallas_call x1, Pallas kernels, on_device(): pl.pallas_call(functools.partial(sweep_kernel, dims), out_shape=(pltpu.VM...  58.3 us
    pallas_call x1, Pallas kernels, on_device(): pl.pallas_call(functools.partial(finish_kernel, dims), out_shape=(jax.Sha...  1.25 us

profile of v10, /device:TPU:1, one launch (start us, length us, event | category | flops | bytes accessed | tf_op | source)
XLA Modules:
  0.0 60.2 jit_solution(13598945876890128501)
XLA Ops:
  0.6 58.3 %shard_map.95 = (f32[2,8,3,64,128]{4,3,2,1,0:T(8,128)S(1)}, f32[2,8,3,64,128]{4,3,2,1,0:T(8,128)S(1)}, f32[3,8,128]{2,1,0:T(8,128)S(1)}, f32[12,2,128]{2,1,0:T(2,128)S(1)}) custom-call(f32[2,3,4,128,128]{4,3,2,1,0:T(8,128)} %spin_hbm.1, f32[3,4,128,128]{3,2,1,0:T(8,128)} %coup_hbm.1, f32[2]{0:T(128)} %beta_hbm.1, s32[2]{0:T(128)} %order_hbm.1, ...), custom_call_target="tpu_custom_call" | custom-call | tf_op jit(solution)/shard_map/pallas_call | solution.py:789
  59.0 1.2 %shard_map.96 = (f32[2,3,4,128,128]{4,3,2,1,0:T(8,128)}, f32[2]{0:T(128)}) custom-call(f32[2,8,3,64,128]{4,3,2,1,0:T(8,128)S(1)} %get-tuple-element.6.evened, f32[2,8,3,64,128]{4,3,2,1,0:T(8,128)S(1)} %get-tuple-element.7.rbuf, f32[3,8,128]{2,1,0:T(8,128)S(1)} %get-tuple-element.8.trecv, f32[12,2,128]{2,1,0:T(2,128)S(1)} %get-tuple-element.9.ebuf), custom_call_target="tpu_custom_call" | custom-call | tf_op jit(solution)/shard_map/pallas_call | solution.py:840
